TPU v7x, 128 devices: a whole 4x4x4 slice. The times are simulated.
128 devices in a mesh: tm: 32 (over y, x, core), space: 4 (over z).
Axes of the slice: x: 4, y: 4, z: 4, core: 2. Of those that a mesh axis runs over, the one named last changes fastest.
Arguments:
- previous_end: float32 [32, 16, 256, 256], P('tm', 'space'), may hold values from -6 to 6
- source: float32 [32, 16, 256, 256], P('tm', 'space'), may hold values from -4 to 4
- rate: float32 [16, 256, 256], P('space'), may hold values from 0.05 to 0.8
Outputs:
- fine_nodes: float32 [32, 2, 16, 256, 256], P('tm', None, 'space')
All inputs are finite; a program needn't handle non-finite values.
Results may differ from a plain program's by a relative error of at most 0.00026.
Values sent between devices are 32-bit elements; how exact they have to be, the bound alone decides.
A program may use at most 128 MiB of HBM per device.

v0:
```python
import jax
import jax.numpy as jnp
from jax import lax
from jax.sharding import Mesh
from jax.sharding import PartitionSpec as P

TM = ("tm_0", "tm_1", "tm_2")


diffusion = 0.1
speed_z = 0.4
speed_x = 0.3
speed_y = 0.2
weights_one = (5.0 / 24.0, 1.0 / 3.0, -1.0 / 24.0)
weights_two = (-1.0 / 24.0, 1.0 / 3.0, 5.0 / 24.0)


def spread(array, axes, root):
    array = jnp.where(lax.axis_index(axes) == root, array, jnp.zeros_like(array))
    for axis in axes:
        array = lax.psum(array, axis)
    return array


def padded_2(array, sides, width):
    for axis, dim in sides:
        size, length = (lax.axis_size(axis), array.shape[dim])
        up = [(i, (i + 1) % size) for i in range(size - 1)]
        down = [(j, i) for i, j in up]
        last = lax.slice_in_dim(array, length - width, length, axis=dim)
        first = lax.slice_in_dim(array, 0, width, axis=dim)
        before = lax.ppermute(last, axis, up)
        after = lax.ppermute(first, axis, down)
        array = jnp.concatenate([before, array, after], axis=dim)
    return array


def laid_out(tiles, dim):
    lengths = list(tiles.shape[1:])
    lengths[dim] *= tiles.shape[0]
    return jnp.moveaxis(tiles, 0, dim).reshape(lengths)


def stacked_from(array, axes, turns):
    tiles = array
    for k in turns:
        tiles = lax.all_gather(tiles, axes[k])
    done = turns[::-1]
    back = [done.index(k) for k in range(len(axes))]
    tiles = tiles.transpose(*back, *range(len(axes), tiles.ndim))
    return tiles.reshape(-1, *array.shape)


def gathered_by_axis(array, axes, turns, dim):
    return laid_out(stacked_from(array, axes, turns), dim)


def tendency(padded, rate_field, source_term, spacing):
    middle = padded[..., 1:-1, :, :]
    upper_z = padded[..., 2:, :, :]
    lower_z = padded[..., :-2, :, :]
    plus_x = jnp.roll(middle, -1, axis=-2)
    minus_x = jnp.roll(middle, 1, axis=-2)
    plus_y = jnp.roll(middle, -1, axis=-1)
    minus_y = jnp.roll(middle, 1, axis=-1)
    laplacian = (upper_z + lower_z + plus_x + minus_x + plus_y + minus_y - 6.0 * middle) / (
        spacing * spacing
    )
    transport = (
        speed_z * (upper_z - lower_z) + speed_x * (plus_x - minus_x) + speed_y * (plus_y - minus_y)
    ) / (2.0 * spacing)
    return (
        diffusion * laplacian
        - transport
        + rate_field * middle / (1.0 + middle * middle)
        + source_term
    )


def pair_table(count):
    fine_index = jnp.arange(count, dtype=jnp.int32)[:, None]
    coarse_index = jnp.arange(count // 2, dtype=jnp.int32)[None, :]
    return (fine_index // 2 == coarse_index).astype(jnp.float32)


def restrict(field):
    count_z, count_x, count_y = field.shape[-3:]
    paired = field.reshape(field.shape[:-3] + (count_z // 2, 2, count_x, count_y))
    summed_z = paired[..., 0, :, :] + paired[..., 1, :, :]
    summed_y = jnp.einsum(
        "...xy,yb->...xb", summed_z, pair_table(count_y), precision=lax.Precision.HIGHEST
    )
    summed_x = jnp.einsum(
        "...xb,xa->...ab", summed_y, pair_table(count_x), precision=lax.Precision.HIGHEST
    )
    return 0.125 * summed_x


def inject(coarse):
    count_x, count_y = coarse.shape[-2:]
    along_y = jnp.einsum(
        "...ab,yb->...ay", coarse, pair_table(2 * count_y), precision=lax.Precision.HIGHEST
    )
    along_x = jnp.einsum(
        "...ay,xa->...xy", along_y, pair_table(2 * count_x), precision=lax.Precision.HIGHEST
    )
    return jnp.repeat(along_x, 2, axis=-3)


def pick(stacked, index):
    return lax.dynamic_index_in_dim(stacked, index, 0, keepdims=False)


def broadcast_seed(warm):
    return spread(warm, TM, lax.axis_size(TM) - 1)


def widen(stacked):
    return padded_2(stacked, (("space", 1),), 1)


def coarse_deep(start, rate_c, source_c, rate_wide, source_wide):
    padded = padded_2(start, (("space", 0),), 2)
    first_wide = padded[1:-1] + 0.5 * tendency(padded, rate_wide, source_wide, 2.0)
    count_z = start.shape[0]
    global_z = lax.axis_index("space") * count_z - 1 + jnp.arange(count_z + 2, dtype=jnp.int32)
    inside = (global_z >= 0) & (global_z < count_z * lax.axis_size("space"))
    first_wide = jnp.where(inside[:, None, None], first_wide, 0.0)
    second = first_wide[1:-1] + 0.5 * tendency(first_wide, rate_c, source_c, 2.0)
    return (first_wide[1:-1], second)


def coarse_pair(start, stacked, wide, index):
    return coarse_deep(start, stacked[0], pick(stacked, index), wide[0], pick(wide, index))


def shards(previous_end, source, rate):
    warm = previous_end[0]
    own_source = source[0]
    rank = lax.axis_index(TM)
    turns = lax.axis_size(TM) - 1
    rate_c = restrict(rate)
    source_c = restrict(own_source)
    restart = broadcast_seed(warm)
    restart_c = restrict(restart)
    all_sources = gathered_by_axis(source_c[None], (("tm_0", "tm_1"), "tm_2"), (0, 1), 0)
    stacked = jnp.concatenate([rate_c[None], all_sources], axis=0)
    wide = widen(stacked)

    def turn(step, value):
        first, second = coarse_pair(value, stacked, wide, step + 1)
        return jnp.where(step < rank, second, value)

    start = lax.fori_loop(0, turns, turn, restart_c)
    first, second = coarse_pair(start, stacked, wide, rank + 1)
    warm_c = restrict(warm)
    guess = jnp.stack(
        [
            restart + inject(start - restart_c),
            warm + inject(first - warm_c),
            warm + inject(second - warm_c),
        ]
    )
    padded = padded_2(guess, (("space", 1),), 1)
    images = tendency(padded, rate, own_source, 1.0)
    node_one = guess[0] + (
        weights_one[0] * images[0] + weights_one[1] * images[1] + weights_one[2] * images[2]
    )
    padded_one = padded_2(node_one, (("space", 0),), 1)
    again = tendency(padded_one, rate, own_source, 1.0)
    node_two = (
        node_one
        + 0.5 * (again - images[1])
        + (weights_two[0] * images[0] + weights_two[1] * images[1] + weights_two[2] * images[2])
    )
    return jnp.stack([node_one, node_two])[None]


def solution(mesh):
    torus = Mesh(
        mesh.devices.reshape(4, 4, 2, mesh.shape["space"]), ("tm_0", "tm_1", "tm_2", "space")
    )
    placed = (P(TM, "space", None, None), P(TM, "space", None, None), P("space", None, None))
    return jax.shard_map(
        shards,
        mesh=torus,
        in_specs=placed,
        out_specs=P(TM, None, "space", None, None),
        check_vma=False,
    )
```

profile of v0, /device:TPU:0, one launch (start us, length us, event | category | flops | bytes accessed | tf_op | source)
XLA Modules:
  0.0 596.0 jit_solution(7642513160581206992)
XLA Ops:
  11.3 54.3 %all-gather.5.cloned.1.call-done = f32[32,128,128]{2,1,0:T(8,128)} async-done(((f32[2,128,128]{2,1,0:T(8,128)}), f32[32,128,128]{2,1,0:T(8,128)}) %all-gather.5.cloned.1.call-update) | async-done | bytes 2097168 | tf_op jit(solution)/shard_map/all_gather | solution.py:47
  67.4 14.5 %all-gather.7.cloned.1.call-done = f32[32,1,2,128,128]{4,3,2,1,0:T(8,128)} async-done(((f32[16,1,2,128,128]{4,3,2,1,0:T(8,128)}), f32[32,1,2,128,128]{4,3,2,1,0:T(8,128)}) %all-gather.7.cloned.1.call-update) | async-done | bytes 4194320 | tf_op jit(solution)/shard_map/all_gather | solution.py:47
  82.0 2.7 copy.23
  84.7 2.5 fusion.8
  87.9 4.9 collective-permute-start.2
  94.2 20.3 %all-reduce.6.cloned.1.call-done = f32[4,256,256]{2,1,0:T(8,128)} async-done(((f32[4,256,256]{2,1,0:T(8,128)}), f32[4,256,256]{2,1,0:T(8,128)}) %all-reduce.6.cloned.1.call-update) | async-done | bytes 1048592 | tf_op jit(solution)/shard_map/psum | solution.py:21
  115.3 25.0 %all-reduce.8.cloned.1.call-done = f32[4,256,256]{2,1,0:T(8,128)} async-done(((f32[4,256,256]{2,1,0:T(8,128)}), f32[4,256,256]{2,1,0:T(8,128)}) %all-reduce.8.cloned.1.call-update) | async-done | bytes 1048592 | tf_op jit(solution)/shard_map/psum | solution.py:21
  142.3 5.0 pad_maximum_fusion.8
  147.4 5.6 pad_maximum_fusion.9
  153.0 381.2 %while.16 = (s32[]{:T(128)}, f32[2,128,128]{2,1,0:T(8,128)S(1)}, s32[]{:T(128)}, f32[33,4,128,128]{3,2,1,0:T(8,128)}, f32[2,128,128]{2,1,0:T(8,128)S(1)}, /*inde...) while((s32[]{:T(128)}, f32[2,128,128]{2,1,0:T(8,128)S(1)}, ...), condition=%wide.region_4.5_spmd, body=%wide.region_3.4_spmd.sunk | while | flops 3047450 | bytes 9568569 | solution.py:154
  153.0 3.7 collective-permute-start
  159.9 4.1 collective-permute-done.1
  167.1 3.5 collective-permute-start
  173.2 4.3 collective-permute-done.1
  180.6 3.2 collective-permute-start
  186.4 4.3 collective-permute-done.1
  198.3 4.3 collective-permute-done.1
  210.3 4.3 collective-permute-done.1
  222.3 4.3 collective-permute-done.1
  229.8 1.9 collective-permute-start
  234.3 4.3 collective-permute-done.1
  246.2 4.3 collective-permute-done.1
  258.4 4.6 collective-permute-done.1
  269.2 2.5 collective-permute-done
  271.8 4.1 collective-permute-done.1
  279.0 2.2 collective-permute-start
  284.3 4.1 collective-permute-done.1
  291.5 2.2 collective-permute-start
  296.3 4.3 collective-permute-done.1
  308.3 4.3 collective-permute-done.1
  320.2 4.3 collective-permute-done.1
  327.7 1.9 collective-permute-start
  332.2 4.3 collective-permute-done.1
  344.2 4.3 collective-permute-done.1
  356.1 4.3 collective-permute-done.1
  363.6 1.9 collective-permute-start
  368.1 4.3 collective-permute-done.1
  380.1 4.6 collective-permute-done.1
  390.8 2.2 collective-permute-done
  393.1 4.6 collective-permute-done.1
  405.6 4.1 collective-permute-done.1
  412.9 2.2 collective-permute-start
  417.7 4.3 collective-permute-done.1
  429.6 4.3 collective-permute-done.1
  437.1 1.9 collective-permute-start
  441.6 4.3 collective-permute-done.1
  453.6 4.3 collective-permute-done.1
  465.5 4.3 collective-permute-done.1
  477.5 4.3 collective-permute-done.1
  489.5 4.3 collective-permute-done.1
  501.4 5.3 collective-permute-done.1
  509.9 2.2 collective-permute-start
  514.7 4.3 collective-permute-done.1
  526.6 4.3 collective-permute-done.1
  535.8 4.6 collective-permute-start.4
  548.7 4.4 collective-permute-start.7
  554.6 2.2 fusion.138
  557.9 4.7 collective-permute-done.7
  562.6 4.4 collective-permute-done.6
  567.9 6.1 %add_add_fusion = f32[3,4,256,256]{3,2,1,0:T(8,128)S(1)} fusion(f32[3,4,256,255]{3,2,1,0:T(8,128)S(1)} %get-tuple-element.228, f32[3,4,256,1]{3,2,1,0:T(8,128)} %get-tuple-element.230, f32[3,4,256,1]{3,2,1,0:T(8,128)} %get-tuple-element.229, f32[3,4,256,255]{3,2,1,0:T(8,128)S(1)} %get-tuple-element.227, f32[3,4,255,256]{3,2,1,0:T(8,128)S(1)} %get-tuple-element.224, ...), kind=kLoop, calls=%fused_computation.46 | loop fusion | flops 28311552 | bytes 22544384 | tf_op jit(solution)/shard_map/add | solution.py:73
  574.9 2.2 collective-permute-start.9
  578.6 2.4 collective-permute-done.9
  581.0 4.4 collective-permute-done.8
  585.4 2.0 fusion.14
  (598 shorter events, 238.7 us)
Async XLA Ops:
  7.4 58.3 %all-gather.5.cloned.1.call-start = ((), (), s32[]{:S(2)}) async-start(), calls=%async_computation.3 | async-start | bytes 2228224 | tf_op jit(solution)/shard_map/all_gather | solution.py:47
  10.1 56.5 %all-reduce.4.cloned.1.call-start = ((), (), s32[]{:S(2)}) async-start(), calls=%async_computation | async-start | bytes 2097152 | tf_op jit(solution)/shard_map/psum | solution.py:21
  11.2 70.7 %all-gather.7.cloned.1.call-start = ((), (), s32[]{:S(2)}) async-start(), calls=%async_computation.4 | async-start | bytes 6291456 | tf_op jit(solution)/shard_map/all_gather | solution.py:47
  65.6 48.8 %all-reduce.6.cloned.1.call-start = ((), (), s32[]{:S(2)}) async-start(), calls=%async_computation.1 | async-start | bytes 2097152 | tf_op jit(solution)/shard_map/psum | solution.py:21
  66.6 73.7 %all-reduce.8.cloned.1.call-start = ((), (), s32[]{:S(2)}) async-start(), calls=%async_computation.2 | async-start | bytes 2097152 | tf_op jit(solution)/shard_map/psum | solution.py:21
  87.9 59.4 %collective-permute-start.2 = (f32[33,1,128,128]{3,2,1,0:T(8,128)}, f32[33,1,128,128]{3,2,1,0:T(8,128)}, u32[]{:S(2)}, u32[]{:S(2)}) collective-permute-start(f32[33,1,128,128]{3,2,1,0:T(8,128)} %get-tuple-element.219), channel_id=1, source_target_pairs={{0,1},{1,2},{2,3},{4,5},{5,6},{6,7},{8,9},{9,10},{10,11},{12,13},{... | collective-permute-start | bytes 6488072 | tf_op jit(solution)/shard_map/ppermute | solution.py:32
  92.9 54.5 %collective-permute-start.3 = (f32[33,1,128,128]{3,2,1,0:T(8,128)}, f32[33,1,128,128]{3,2,1,0:T(8,128)}, u32[]{:S(2)}, u32[]{:S(2)}) collective-permute-start(f32[33,1,128,128]{3,2,1,0:T(8,128)} %get-tuple-element.220), channel_id=1, source_target_pairs={{1,0},{2,1},{3,2},{5,4},{6,5},{7,6},{9,8},{10,9},{11,10},{13,12},{... | collective-permute-start | bytes 6488072 | tf_op jit(solution)/shard_map/ppermute | solution.py:33
  153.0 6.9 %collective-permute-start = (f32[2,128,128]{2,1,0:T(8,128)S(1)}, f32[2,128,128]{2,1,0:T(8,128)S(1)}, u32[]{:S(2)}, u32[]{:S(2)}) collective-permute-start(f32[2,128,128]{2,1,0:T(8,128)S(1)} %get-tuple-element.362), channel_id=1, source_target_pairs={{0,1},{1,2},{2,3},{4,5},{5,6},{6,7},{8,9},{9,10},{10,11},{12,13},{... | collective-permute-start | bytes 393224 | tf_op jit(solution)/shard_map/while/body/eval_jaxpr/ppermute | solution.py:32
  156.7 7.3 %collective-permute-start.1 = (f32[2,128,128]{2,1,0:T(8,128)S(1)}, f32[2,128,128]{2,1,0:T(8,128)S(1)}, u32[]{:S(2)}, u32[]{:S(2)}) collective-permute-start(f32[2,128,128]{2,1,0:T(8,128)S(1)} %get-tuple-element.362), channel_id=1, source_target_pairs={{1,0},{2,1},{3,2},{5,4},{6,5},{7,6},{9,8},{10,9},{11,10},{13,12},{... | collective-permute-start | bytes 393224 | tf_op jit(solution)/shard_map/while/body/eval_jaxpr/ppermute | solution.py:33
  167.1 6.0 %collective-permute-start = (f32[2,128,128]{2,1,0:T(8,128)S(1)}, f32[2,128,128]{2,1,0:T(8,128)S(1)}, u32[]{:S(2)}, u32[]{:S(2)}) collective-permute-start(f32[2,128,128]{2,1,0:T(8,128)S(1)} %get-tuple-element.362), channel_id=1, source_target_pairs={{0,1},{1,2},{2,3},{4,5},{5,6},{6,7},{8,9},{9,10},{10,11},{12,13},{... | collective-permute-start | bytes 393224 | tf_op jit(solution)/shard_map/while/body/eval_jaxpr/ppermute | solution.py:32
  170.6 6.9 %collective-permute-start.1 = (f32[2,128,128]{2,1,0:T(8,128)S(1)}, f32[2,128,128]{2,1,0:T(8,128)S(1)}, u32[]{:S(2)}, u32[]{:S(2)}) collective-permute-start(f32[2,128,128]{2,1,0:T(8,128)S(1)} %get-tuple-element.362), channel_id=1, source_target_pairs={{1,0},{2,1},{3,2},{5,4},{6,5},{7,6},{9,8},{10,9},{11,10},{13,12},{... | collective-permute-start | bytes 393224 | tf_op jit(solution)/shard_map/while/body/eval_jaxpr/ppermute | solution.py:33
  180.6 5.7 collective-permute-start
  183.8 6.9 %collective-permute-start.1 = (f32[2,128,128]{2,1,0:T(8,128)S(1)}, f32[2,128,128]{2,1,0:T(8,128)S(1)}, u32[]{:S(2)}, u32[]{:S(2)}) collective-permute-start(f32[2,128,128]{2,1,0:T(8,128)S(1)} %get-tuple-element.362), channel_id=1, source_target_pairs={{1,0},{2,1},{3,2},{5,4},{6,5},{7,6},{9,8},{10,9},{11,10},{13,12},{... | collective-permute-start | bytes 393224 | tf_op jit(solution)/shard_map/while/body/eval_jaxpr/ppermute | solution.py:33
  193.9 4.4 collective-permute-start
  195.8 6.9 %collective-permute-start.1 = (f32[2,128,128]{2,1,0:T(8,128)S(1)}, f32[2,128,128]{2,1,0:T(8,128)S(1)}, u32[]{:S(2)}, u32[]{:S(2)}) collective-permute-start(f32[2,128,128]{2,1,0:T(8,128)S(1)} %get-tuple-element.362), channel_id=1, source_target_pairs={{1,0},{2,1},{3,2},{5,4},{6,5},{7,6},{9,8},{10,9},{11,10},{13,12},{... | collective-permute-start | bytes 393224 | tf_op jit(solution)/shard_map/while/body/eval_jaxpr/ppermute | solution.py:33
  205.8 4.4 collective-permute-start
  207.8 6.9 %collective-permute-start.1 = (f32[2,128,128]{2,1,0:T(8,128)S(1)}, f32[2,128,128]{2,1,0:T(8,128)S(1)}, u32[]{:S(2)}, u32[]{:S(2)}) collective-permute-start(f32[2,128,128]{2,1,0:T(8,128)S(1)} %get-tuple-element.362), channel_id=1, source_target_pairs={{1,0},{2,1},{3,2},{5,4},{6,5},{7,6},{9,8},{10,9},{11,10},{13,12},{... | collective-permute-start | bytes 393224 | tf_op jit(solution)/shard_map/while/body/eval_jaxpr/ppermute | solution.py:33
  219.7 6.9 %collective-permute-start.1 = (f32[2,128,128]{2,1,0:T(8,128)S(1)}, f32[2,128,128]{2,1,0:T(8,128)S(1)}, u32[]{:S(2)}, u32[]{:S(2)}) collective-permute-start(f32[2,128,128]{2,1,0:T(8,128)S(1)} %get-tuple-element.362), channel_id=1, source_target_pairs={{1,0},{2,1},{3,2},{5,4},{6,5},{7,6},{9,8},{10,9},{11,10},{13,12},{... | collective-permute-start | bytes 393224 | tf_op jit(solution)/shard_map/while/body/eval_jaxpr/ppermute | solution.py:33
  229.8 4.4 collective-permute-start
  231.7 6.9 %collective-permute-start.1 = (f32[2,128,128]{2,1,0:T(8,128)S(1)}, f32[2,128,128]{2,1,0:T(8,128)S(1)}, u32[]{:S(2)}, u32[]{:S(2)}) collective-permute-start(f32[2,128,128]{2,1,0:T(8,128)S(1)} %get-tuple-element.362), channel_id=1, source_target_pairs={{1,0},{2,1},{3,2},{5,4},{6,5},{7,6},{9,8},{10,9},{11,10},{13,12},{... | collective-permute-start | bytes 393224 | tf_op jit(solution)/shard_map/while/body/eval_jaxpr/ppermute | solution.py:33
  241.7 4.4 collective-permute-start
  243.7 6.9 %collective-permute-start.1 = (f32[2,128,128]{2,1,0:T(8,128)S(1)}, f32[2,128,128]{2,1,0:T(8,128)S(1)}, u32[]{:S(2)}, u32[]{:S(2)}) collective-permute-start(f32[2,128,128]{2,1,0:T(8,128)S(1)} %get-tuple-element.362), channel_id=1, source_target_pairs={{1,0},{2,1},{3,2},{5,4},{6,5},{7,6},{9,8},{10,9},{11,10},{13,12},{... | collective-permute-start | bytes 393224 | tf_op jit(solution)/shard_map/while/body/eval_jaxpr/ppermute | solution.py:33
  253.7 4.6 collective-permute-start
  255.6 7.4 %collective-permute-start.1 = (f32[2,128,128]{2,1,0:T(8,128)S(1)}, f32[2,128,128]{2,1,0:T(8,128)S(1)}, u32[]{:S(2)}, u32[]{:S(2)}) collective-permute-start(f32[2,128,128]{2,1,0:T(8,128)S(1)} %get-tuple-element.362), channel_id=1, source_target_pairs={{1,0},{2,1},{3,2},{5,4},{6,5},{7,6},{9,8},{10,9},{11,10},{13,12},{... | collective-permute-start | bytes 393224 | tf_op jit(solution)/shard_map/while/body/eval_jaxpr/ppermute | solution.py:33
  266.2 5.5 collective-permute-start
  267.9 8.0 %collective-permute-start.1 = (f32[2,128,128]{2,1,0:T(8,128)S(1)}, f32[2,128,128]{2,1,0:T(8,128)S(1)}, u32[]{:S(2)}, u32[]{:S(2)}) collective-permute-start(f32[2,128,128]{2,1,0:T(8,128)S(1)} %get-tuple-element.362), channel_id=1, source_target_pairs={{1,0},{2,1},{3,2},{5,4},{6,5},{7,6},{9,8},{10,9},{11,10},{13,12},{... | collective-permute-start | bytes 393224 | tf_op jit(solution)/shard_map/while/body/eval_jaxpr/ppermute | solution.py:33
  279.0 5.2 collective-permute-start
  281.2 7.1 %collective-permute-start.1 = (f32[2,128,128]{2,1,0:T(8,128)S(1)}, f32[2,128,128]{2,1,0:T(8,128)S(1)}, u32[]{:S(2)}, u32[]{:S(2)}) collective-permute-start(f32[2,128,128]{2,1,0:T(8,128)S(1)} %get-tuple-element.362), channel_id=1, source_target_pairs={{1,0},{2,1},{3,2},{5,4},{6,5},{7,6},{9,8},{10,9},{11,10},{13,12},{... | collective-permute-start | bytes 393224 | tf_op jit(solution)/shard_map/while/body/eval_jaxpr/ppermute | solution.py:33
  291.5 4.7 collective-permute-start
  293.7 6.9 %collective-permute-start.1 = (f32[2,128,128]{2,1,0:T(8,128)S(1)}, f32[2,128,128]{2,1,0:T(8,128)S(1)}, u32[]{:S(2)}, u32[]{:S(2)}) collective-permute-start(f32[2,128,128]{2,1,0:T(8,128)S(1)} %get-tuple-element.362), channel_id=1, source_target_pairs={{1,0},{2,1},{3,2},{5,4},{6,5},{7,6},{9,8},{10,9},{11,10},{13,12},{... | collective-permute-start | bytes 393224 | tf_op jit(solution)/shard_map/while/body/eval_jaxpr/ppermute | solution.py:33
  303.8 4.4 collective-permute-start
  305.7 6.9 %collective-permute-start.1 = (f32[2,128,128]{2,1,0:T(8,128)S(1)}, f32[2,128,128]{2,1,0:T(8,128)S(1)}, u32[]{:S(2)}, u32[]{:S(2)}) collective-permute-start(f32[2,128,128]{2,1,0:T(8,128)S(1)} %get-tuple-element.362), channel_id=1, source_target_pairs={{1,0},{2,1},{3,2},{5,4},{6,5},{7,6},{9,8},{10,9},{11,10},{13,12},{... | collective-permute-start | bytes 393224 | tf_op jit(solution)/shard_map/while/body/eval_jaxpr/ppermute | solution.py:33
  315.8 4.4 collective-permute-start
  317.7 6.9 %collective-permute-start.1 = (f32[2,128,128]{2,1,0:T(8,128)S(1)}, f32[2,128,128]{2,1,0:T(8,128)S(1)}, u32[]{:S(2)}, u32[]{:S(2)}) collective-permute-start(f32[2,128,128]{2,1,0:T(8,128)S(1)} %get-tuple-element.362), channel_id=1, source_target_pairs={{1,0},{2,1},{3,2},{5,4},{6,5},{7,6},{9,8},{10,9},{11,10},{13,12},{... | collective-permute-start | bytes 393224 | tf_op jit(solution)/shard_map/while/body/eval_jaxpr/ppermute | solution.py:33
  327.7 4.4 collective-permute-start
  329.6 6.9 %collective-permute-start.1 = (f32[2,128,128]{2,1,0:T(8,128)S(1)}, f32[2,128,128]{2,1,0:T(8,128)S(1)}, u32[]{:S(2)}, u32[]{:S(2)}) collective-permute-start(f32[2,128,128]{2,1,0:T(8,128)S(1)} %get-tuple-element.362), channel_id=1, source_target_pairs={{1,0},{2,1},{3,2},{5,4},{6,5},{7,6},{9,8},{10,9},{11,10},{13,12},{... | collective-permute-start | bytes 393224 | tf_op jit(solution)/shard_map/while/body/eval_jaxpr/ppermute | solution.py:33
  339.7 4.4 collective-permute-start
  341.6 6.9 %collective-permute-start.1 = (f32[2,128,128]{2,1,0:T(8,128)S(1)}, f32[2,128,128]{2,1,0:T(8,128)S(1)}, u32[]{:S(2)}, u32[]{:S(2)}) collective-permute-start(f32[2,128,128]{2,1,0:T(8,128)S(1)} %get-tuple-element.362), channel_id=1, source_target_pairs={{1,0},{2,1},{3,2},{5,4},{6,5},{7,6},{9,8},{10,9},{11,10},{13,12},{... | collective-permute-start | bytes 393224 | tf_op jit(solution)/shard_map/while/body/eval_jaxpr/ppermute | solution.py:33
  351.7 4.4 collective-permute-start
  353.6 6.9 %collective-permute-start.1 = (f32[2,128,128]{2,1,0:T(8,128)S(1)}, f32[2,128,128]{2,1,0:T(8,128)S(1)}, u32[]{:S(2)}, u32[]{:S(2)}) collective-permute-start(f32[2,128,128]{2,1,0:T(8,128)S(1)} %get-tuple-element.362), channel_id=1, source_target_pairs={{1,0},{2,1},{3,2},{5,4},{6,5},{7,6},{9,8},{10,9},{11,10},{13,12},{... | collective-permute-start | bytes 393224 | tf_op jit(solution)/shard_map/while/body/eval_jaxpr/ppermute | solution.py:33
  365.6 6.9 %collective-permute-start.1 = (f32[2,128,128]{2,1,0:T(8,128)S(1)}, f32[2,128,128]{2,1,0:T(8,128)S(1)}, u32[]{:S(2)}, u32[]{:S(2)}) collective-permute-start(f32[2,128,128]{2,1,0:T(8,128)S(1)} %get-tuple-element.362), channel_id=1, source_target_pairs={{1,0},{2,1},{3,2},{5,4},{6,5},{7,6},{9,8},{10,9},{11,10},{13,12},{... | collective-permute-start | bytes 393224 | tf_op jit(solution)/shard_map/while/body/eval_jaxpr/ppermute | solution.py:33
  377.5 7.1 %collective-permute-start.1 = (f32[2,128,128]{2,1,0:T(8,128)S(1)}, f32[2,128,128]{2,1,0:T(8,128)S(1)}, u32[]{:S(2)}, u32[]{:S(2)}) collective-permute-start(f32[2,128,128]{2,1,0:T(8,128)S(1)} %get-tuple-element.362), channel_id=1, source_target_pairs={{1,0},{2,1},{3,2},{5,4},{6,5},{7,6},{9,8},{10,9},{11,10},{13,12},{... | collective-permute-start | bytes 393224 | tf_op jit(solution)/shard_map/while/body/eval_jaxpr/ppermute | solution.py:33
  387.8 5.3 collective-permute-start
  389.5 8.3 %collective-permute-start.1 = (f32[2,128,128]{2,1,0:T(8,128)S(1)}, f32[2,128,128]{2,1,0:T(8,128)S(1)}, u32[]{:S(2)}, u32[]{:S(2)}) collective-permute-start(f32[2,128,128]{2,1,0:T(8,128)S(1)} %get-tuple-element.362), channel_id=1, source_target_pairs={{1,0},{2,1},{3,2},{5,4},{6,5},{7,6},{9,8},{10,9},{11,10},{13,12},{... | collective-permute-start | bytes 393224 | tf_op jit(solution)/shard_map/while/body/eval_jaxpr/ppermute | solution.py:33
  400.9 4.7 collective-permute-start
  402.6 7.1 %collective-permute-start.1 = (f32[2,128,128]{2,1,0:T(8,128)S(1)}, f32[2,128,128]{2,1,0:T(8,128)S(1)}, u32[]{:S(2)}, u32[]{:S(2)}) collective-permute-start(f32[2,128,128]{2,1,0:T(8,128)S(1)} %get-tuple-element.362), channel_id=1, source_target_pairs={{1,0},{2,1},{3,2},{5,4},{6,5},{7,6},{9,8},{10,9},{11,10},{13,12},{... | collective-permute-start | bytes 393224 | tf_op jit(solution)/shard_map/while/body/eval_jaxpr/ppermute | solution.py:33
  412.9 4.7 collective-permute-start
  415.1 6.9 %collective-permute-start.1 = (f32[2,128,128]{2,1,0:T(8,128)S(1)}, f32[2,128,128]{2,1,0:T(8,128)S(1)}, u32[]{:S(2)}, u32[]{:S(2)}) collective-permute-start(f32[2,128,128]{2,1,0:T(8,128)S(1)} %get-tuple-element.362), channel_id=1, source_target_pairs={{1,0},{2,1},{3,2},{5,4},{6,5},{7,6},{9,8},{10,9},{11,10},{13,12},{... | collective-permute-start | bytes 393224 | tf_op jit(solution)/shard_map/while/body/eval_jaxpr/ppermute | solution.py:33
  427.1 6.9 %collective-permute-start.1 = (f32[2,128,128]{2,1,0:T(8,128)S(1)}, f32[2,128,128]{2,1,0:T(8,128)S(1)}, u32[]{:S(2)}, u32[]{:S(2)}) collective-permute-start(f32[2,128,128]{2,1,0:T(8,128)S(1)} %get-tuple-element.362), channel_id=1, source_target_pairs={{1,0},{2,1},{3,2},{5,4},{6,5},{7,6},{9,8},{10,9},{11,10},{13,12},{... | collective-permute-start | bytes 393224 | tf_op jit(solution)/shard_map/while/body/eval_jaxpr/ppermute | solution.py:33
  439.0 6.9 %collective-permute-start.1 = (f32[2,128,128]{2,1,0:T(8,128)S(1)}, f32[2,128,128]{2,1,0:T(8,128)S(1)}, u32[]{:S(2)}, u32[]{:S(2)}) collective-permute-start(f32[2,128,128]{2,1,0:T(8,128)S(1)} %get-tuple-element.362), channel_id=1, source_target_pairs={{1,0},{2,1},{3,2},{5,4},{6,5},{7,6},{9,8},{10,9},{11,10},{13,12},{... | collective-permute-start | bytes 393224 | tf_op jit(solution)/shard_map/while/body/eval_jaxpr/ppermute | solution.py:33
  451.0 6.9 %collective-permute-start.1 = (f32[2,128,128]{2,1,0:T(8,128)S(1)}, f32[2,128,128]{2,1,0:T(8,128)S(1)}, u32[]{:S(2)}, u32[]{:S(2)}) collective-permute-start(f32[2,128,128]{2,1,0:T(8,128)S(1)} %get-tuple-element.362), channel_id=1, source_target_pairs={{1,0},{2,1},{3,2},{5,4},{6,5},{7,6},{9,8},{10,9},{11,10},{13,12},{... | collective-permute-start | bytes 393224 | tf_op jit(solution)/shard_map/while/body/eval_jaxpr/ppermute | solution.py:33
  463.0 6.9 %collective-permute-start.1 = (f32[2,128,128]{2,1,0:T(8,128)S(1)}, f32[2,128,128]{2,1,0:T(8,128)S(1)}, u32[]{:S(2)}, u32[]{:S(2)}) collective-permute-start(f32[2,128,128]{2,1,0:T(8,128)S(1)} %get-tuple-element.362), channel_id=1, source_target_pairs={{1,0},{2,1},{3,2},{5,4},{6,5},{7,6},{9,8},{10,9},{11,10},{13,12},{... | collective-permute-start | bytes 393224 | tf_op jit(solution)/shard_map/while/body/eval_jaxpr/ppermute | solution.py:33
  474.9 6.9 %collective-permute-start.1 = (f32[2,128,128]{2,1,0:T(8,128)S(1)}, f32[2,128,128]{2,1,0:T(8,128)S(1)}, u32[]{:S(2)}, u32[]{:S(2)}) collective-permute-start(f32[2,128,128]{2,1,0:T(8,128)S(1)} %get-tuple-element.362), channel_id=1, source_target_pairs={{1,0},{2,1},{3,2},{5,4},{6,5},{7,6},{9,8},{10,9},{11,10},{13,12},{... | collective-permute-start | bytes 393224 | tf_op jit(solution)/shard_map/while/body/eval_jaxpr/ppermute | solution.py:33
  486.9 6.9 %collective-permute-start.1 = (f32[2,128,128]{2,1,0:T(8,128)S(1)}, f32[2,128,128]{2,1,0:T(8,128)S(1)}, u32[]{:S(2)}, u32[]{:S(2)}) collective-permute-start(f32[2,128,128]{2,1,0:T(8,128)S(1)} %get-tuple-element.362), channel_id=1, source_target_pairs={{1,0},{2,1},{3,2},{5,4},{6,5},{7,6},{9,8},{10,9},{11,10},{13,12},{... | collective-permute-start | bytes 393224 | tf_op jit(solution)/shard_map/while/body/eval_jaxpr/ppermute | solution.py:33
  498.9 7.9 %collective-permute-start.1 = (f32[2,128,128]{2,1,0:T(8,128)S(1)}, f32[2,128,128]{2,1,0:T(8,128)S(1)}, u32[]{:S(2)}, u32[]{:S(2)}) collective-permute-start(f32[2,128,128]{2,1,0:T(8,128)S(1)} %get-tuple-element.362), channel_id=1, source_target_pairs={{1,0},{2,1},{3,2},{5,4},{6,5},{7,6},{9,8},{10,9},{11,10},{13,12},{... | collective-permute-start | bytes 393224 | tf_op jit(solution)/shard_map/while/body/eval_jaxpr/ppermute | solution.py:33
  509.9 4.7 collective-permute-start
  512.1 6.9 %collective-permute-start.1 = (f32[2,128,128]{2,1,0:T(8,128)S(1)}, f32[2,128,128]{2,1,0:T(8,128)S(1)}, u32[]{:S(2)}, u32[]{:S(2)}) collective-permute-start(f32[2,128,128]{2,1,0:T(8,128)S(1)} %get-tuple-element.362), channel_id=1, source_target_pairs={{1,0},{2,1},{3,2},{5,4},{6,5},{7,6},{9,8},{10,9},{11,10},{13,12},{... | collective-permute-start | bytes 393224 | tf_op jit(solution)/shard_map/while/body/eval_jaxpr/ppermute | solution.py:33
  524.1 6.9 %collective-permute-start.1 = (f32[2,128,128]{2,1,0:T(8,128)S(1)}, f32[2,128,128]{2,1,0:T(8,128)S(1)}, u32[]{:S(2)}, u32[]{:S(2)}) collective-permute-start(f32[2,128,128]{2,1,0:T(8,128)S(1)} %get-tuple-element.362), channel_id=1, source_target_pairs={{1,0},{2,1},{3,2},{5,4},{6,5},{7,6},{9,8},{10,9},{11,10},{13,12},{... | collective-permute-start | bytes 393224 | tf_op jit(solution)/shard_map/while/body/eval_jaxpr/ppermute | solution.py:33
  534.5 8.8 %collective-permute-start.5 = (f32[2,128,128]{2,1,0:T(8,128)S(1)}, f32[2,128,128]{2,1,0:T(8,128)S(1)}, u32[]{:S(2)}, u32[]{:S(2)}) collective-permute-start(f32[2,128,128]{2,1,0:T(8,128)S(1)} %get-tuple-element.183), channel_id=1, source_target_pairs={{1,0},{2,1},{3,2},{5,4},{6,5},{7,6},{9,8},{10,9},{11,10},{13,12},{... | collective-permute-start | bytes 393224 | tf_op jit(solution)/shard_map/ppermute | solution.py:33
  535.8 7.5 %collective-permute-start.4 = (f32[2,128,128]{2,1,0:T(8,128)S(1)}, f32[2,128,128]{2,1,0:T(8,128)S(1)}, u32[]{:S(2)}, u32[]{:S(2)}) collective-permute-start(f32[2,128,128]{2,1,0:T(8,128)S(1)} %get-tuple-element.183), channel_id=1, source_target_pairs={{0,1},{1,2},{2,3},{4,5},{5,6},{6,7},{8,9},{9,10},{10,11},{12,13},{... | collective-permute-start | bytes 393224 | tf_op jit(solution)/shard_map/ppermute | solution.py:32
  548.7 13.9 %collective-permute-start.7 = (f32[3,1,256,256]{3,2,1,0:T(8,128)S(1)}, f32[3,1,256,256]{3,2,1,0:T(8,128)S(1)}, u32[]{:S(2)}, u32[]{:S(2)}) collective-permute-start(f32[3,1,256,256]{3,2,1,0:T(8,128)S(1)} %get-tuple-element.221), channel_id=1, source_target_pairs={{0,1},{1,2},{2,3},{4,5},{5,6},{6,7},{8,9},{9,10},{10,11},{12,13},{... | collective-permute-start | bytes 2359304 | tf_op jit(solution)/shard_map/ppermute | solution.py:32
  553.1 13.9 %collective-permute-start.6 = (f32[3,1,256,256]{3,2,1,0:T(8,128)S(1)}, f32[3,1,256,256]{3,2,1,0:T(8,128)S(1)}, u32[]{:S(2)}, u32[]{:S(2)}) collective-permute-start(f32[3,1,256,256]{3,2,1,0:T(8,128)S(1)} %get-tuple-element.222), channel_id=1, source_target_pairs={{1,0},{2,1},{3,2},{5,4},{6,5},{7,6},{9,8},{10,9},{11,10},{13,12},{... | collective-permute-start | bytes 2359304 | tf_op jit(solution)/shard_map/ppermute | solution.py:33
  574.9 6.0 %collective-permute-start.9 = (f32[1,256,256]{2,1,0:T(8,128)S(1)}, f32[1,256,256]{2,1,0:T(8,128)S(1)}, u32[]{:S(2)}, u32[]{:S(2)}) collective-permute-start(f32[1,256,256]{2,1,0:T(8,128)S(1)} %get-tuple-element.231), channel_id=1, source_target_pairs={{0,1},{1,2},{2,3},{4,5},{5,6},{6,7},{8,9},{9,10},{10,11},{12,13},{... | collective-permute-start | bytes 786440 | tf_op jit(solution)/shard_map/ppermute | solution.py:32
  577.1 8.3 %collective-permute-start.8 = (f32[1,256,256]{2,1,0:T(8,128)S(1)}, f32[1,256,256]{2,1,0:T(8,128)S(1)}, u32[]{:S(2)}, u32[]{:S(2)}) collective-permute-start(f32[1,256,256]{2,1,0:T(8,128)S(1)} %get-tuple-element.232), channel_id=1, source_target_pairs={{1,0},{2,1},{3,2},{5,4},{6,5},{7,6},{9,8},{10,9},{11,10},{13,12},{... | collective-permute-start | bytes 786440 | tf_op jit(solution)/shard_map/ppermute | solution.py:33
  (21 other events, 549.6 us)
Sparse Core Ops, SparseCore 0:
  10.3 55.2 all-gather.4
  67.3 14.6 all-gather.6
  114.6 25.6 all-reduce.7
Sparse Core Ops, SparseCore 1:
  12.9 53.6 all-reduce.3
  68.8 45.6 all-reduce.5
where the time goes:
time: 599 us; the launch traced here: 596 us
  waiting for transfers between devices  307 us (51%)
  starting transfers between devices  126 us (21%)
  other arithmetic  107 us (18%)
  local copies, waits for them, and re-layouts  28 us (5%)
  between operations  15.1 us (3%)
  matrix products  8.64 us (1%)
    ppermute x35, waiting for transfers between devices, padded_2(): after = lax.ppermute(first, axis, down)  143 us
    ppermute x35, starting transfers between devices, padded_2(): before = lax.ppermute(last, axis, up)  80.5 us
    all_gather x2, waiting for transfers between devices, stacked_from(): tiles = lax.all_gather(tiles, axes[k])  68.8 us
    ppermute x35, waiting for transfers between devices, padded_2(): before = lax.ppermute(last, axis, up)  48.7 us
    select_n x32, other arithmetic, coarse_deep(): first_wide = jnp.where(inside[:, None, None], first_wide, 0.0)  46.3 us
    psum x3, waiting for transfers between devices, spread(): array = lax.psum(array, axis)  46.1 us
    ppermute x35, starting transfers between devices, padded_2(): after = lax.ppermute(first, axis, down)  45.4 us
    select_n x31, other arithmetic, turn(): return jnp.where(step < rank, second, value)  34.9 us
  transfers between devices with their start and end apart: 75, of which 72 were waited for; matrix products, arithmetic and copies ran while one was open for 4% of the time, Pallas kernels for 0%

commit v1 on v0

v1 whole, which is shorter than its diff:
```python
import jax
import jax.numpy as jnp
from jax import lax
from jax.experimental import pallas as pl
from jax.experimental.pallas import tpu as pltpu
from jax.sharding import Mesh
from jax.sharding import PartitionSpec as P

TM = ("tm_0", "tm_1", "tm_2")
AXES = TM + ("space",)
MESH = pl.DeviceIdType.MESH
F32 = jnp.float32

diffusion = 0.1
speed_z = 0.4
speed_x = 0.3
speed_y = 0.2
weights_one = (5.0 / 24.0, 1.0 / 3.0, -1.0 / 24.0)
weights_two = (-1.0 / 24.0, 1.0 / 3.0, 5.0 / 24.0)


def stencil_weights(spacing):
    d = diffusion / (spacing * spacing)
    out = [-6.0 * d]
    for speed in (speed_z, speed_x, speed_y):
        out += [d - speed / (2.0 * spacing), d + speed / (2.0 * spacing)]
    return out


def pair_table(fine, coarse):
    rows = lax.broadcasted_iota(jnp.int32, (fine, coarse), 0) // 2
    columns = lax.broadcasted_iota(jnp.int32, (fine, coarse), 1)
    return (rows == columns).astype(F32)


def pooled(total, pair, scratch):
    scratch[...] = jnp.dot(
        total, pair, precision=lax.Precision.HIGHEST, preferred_element_type=F32
    )
    return scratch[pl.ds(0, 128, stride=2), :] + scratch[pl.ds(1, 128, stride=2), :]


def coarse_stage(src, dst, rate, source, row, tiles):
    w = [0.5 * v for v in stencil_weights(2.0)]
    for j in tiles:
        r = 8 + 8 * j
        below = src[0, pl.ds(r, 8), :]
        here = src[1, pl.ds(r, 8), :]
        for k in range(1, 9):
            above = src[k + 1, pl.ds(r, 8), :]
            out = (1.0 + w[0]) * here + source[k - 1, pl.ds(row + 8 * j, 8), :]
            out += w[1] * above + w[2] * below
            out += w[3] * src[k, pl.ds(r + 1, 8), :] + w[4] * src[k, pl.ds(r - 1, 8), :]
            out += w[5] * pltpu.roll(here, 127, 1) + w[6] * pltpu.roll(here, 1, 1)
            out += rate[k - 1, pl.ds(8 * j, 8), :] * here * pl.reciprocal(1.0 + here * here)
            dst[k, pl.ds(r, 8), :] = out
            below, here = here, above


N_SEND = 160


def chain_kernel(
    prev, source, rate,
    states, restart, prev_lo, prev_hi, source_lo, source_hi, rate_lo, rate_hi,
    fine_s, fine_r, fine_p, half, own, buf, rate_c, seed, state_a, state_b,
    edge_out, edge_in, found,
    load_sem, send_sem, slot_sem, seed_sem, rate_sem, edge_sem, state_sem, halo_sem, restart_sem,
):
    y, x, c, z = (lax.axis_index(name) for name in AXES)
    chip = y * 4 + x
    mine = chip * 2 + c
    slab = 2 * z + c
    is_last = mine == 31
    root_chip = chip == 15
    partner = (y, x, 1 - c, z)
    waits = []

    def guarded(cond, action):
        if cond is None:
            action()
        else:
            pl.when(cond)(action)

    def send(src, dst, sem, device, cond=None):
        index = len(waits)

        def build():
            return pltpu.make_async_remote_copy(
                src_ref=src, dst_ref=dst, send_sem=send_sem.at[index], recv_sem=sem,
                device_id=device, device_id_type=MESH,
            )

        waits.append((cond, lambda: build().wait_send()))
        guarded(cond, lambda: build().start())

    def arrived(view, sem, cond=None):
        def wait():
            pltpu.make_async_remote_copy(
                src_ref=view, dst_ref=view, send_sem=send_sem.at[0], recv_sem=sem,
                device_id=partner, device_id_type=MESH,
            ).wait_recv()

        guarded(cond, wait)

    def turned(value):
        return lax.rem(value + 8, 4)

    def first(step):
        return (turned(y + step * c), turned(x + step * (1 - c)), c, z)

    def second(step):
        return (turned(y + step * (1 - c)), turned(x + step * c), c, z)

    def slot(da, db):
        return (turned(y + da * c + db * (1 - c)) * 4 + turned(x + da * (1 - c) + db * c)) * 2 + c

    load_p = pltpu.make_async_copy(prev, fine_p, load_sem.at[0])
    load_s = pltpu.make_async_copy(source, fine_s, load_sem.at[1])
    load_r = pltpu.make_async_copy(rate, fine_r, load_sem.at[2])
    pl.when(is_last)(load_p.start)
    load_s.start()
    load_r.start()
    barrier = pltpu.get_barrier_semaphore()
    peers = [first(1), first(-1), second(1), second(-1)]
    peers += [(y, x, c, turned(z + d)) for d in (1, 2, 3)]
    peers += [(y, x, 1 - c, turned(z + d)) for d in (0, 1, 2, 3)]
    for device in peers:
        pl.semaphore_signal(barrier, inc=1, device_id=device, device_id_type=MESH)

    pair = pair_table(256, 128)

    def restrict(fine, index, scale):
        for k in range(2):
            total = scale * pooled(fine[2 * k] + fine[2 * k + 1], pair, half)
            own[index, k, pl.ds(16, 128), :] = total
            own[index, k, pl.ds(0, 16), :] = total[112:128]
            own[index, k, pl.ds(144, 16), :] = total[0:16]

    def restrict_last():
        load_p.wait()
        restrict(fine_p, 2, 0.125)

    pl.when(is_last)(restrict_last)
    load_s.wait()
    restrict(fine_s, 0, 0.0625)
    pl.semaphore_wait(barrier, len(peers))

    layers = pl.ds(2 * z, 2)
    rows = pl.ds(16 * c, 48)

    for d in (0, 1, 2, 3):
        to = turned(z + d)
        for core in (0, 1):
            if d or not core:
                send(
                    own.at[2, :, pl.ds(32 * to + 16 * core, 48), :], seed.at[layers],
                    seed_sem, (y, x, core, to), is_last,
                )

    def seed_self():
        seed[layers] = own[2, :, pl.ds(32 * z + 16, 48), :]

    pl.when(is_last)(seed_self)

    for d in (1, 3, 2):
        to = turned(z + d)
        send(
            own.at[0, :, pl.ds(32 * to, 64), :], buf.at[mine, layers], slot_sem.at[mine],
            (y, x, c, to),
        )
    buf[mine, layers] = own[0, :, pl.ds(32 * z, 64), :]
    load_r.wait()
    restrict(fine_r, 1, 0.0625)
    for d in (1, 3, 2):
        to = turned(z + d)
        send(
            own.at[1, :, pl.ds(32 * to + 16 * c, 48), :], rate_c.at[layers], rate_sem,
            (y, x, c, to),
        )
    rate_c[layers] = own[1, :, pl.ds(32 * z + 16 * c, 48), :]

    part = pl.ds(2 + 2 * c, 2)
    local = pltpu.make_async_copy(fine_p, restart.at[pl.ds(2, 4)], load_sem.at[0])

    def place_last():
        local.start()
        local.wait()

    send(fine_p.at[pl.ds(0, 2)], restart.at[pl.ds(2, 2)], restart_sem.at[0], partner, is_last)
    pl.when(is_last)(place_last)

    along = x * (1 - c) + y * c
    across = y * (1 - c) + x * c
    da, db = turned(along + 1), turned(across + 1)
    near = (db == 0) & ((da == 1) | (da == 3))
    side = (db == 1) | (db == 3)
    is_root = (da == 0) & (db == 0)

    class Item:
        def __init__(self, full, halves, sem):
            self.full, self.halves, self.sem = full, halves, sem

        def go(self, device, cond):
            send(self.full, self.full, self.sem, device, cond)

        def root(self, ready):
            ready()
            for device in (first(1), first(-1), second(1), second(-1)):
                self.go(device, is_root)

        def step_near(self):
            arrived(self.full, self.sem, near)
            view = self.halves(jnp.where(da == 1, 0, 1))
            send(view, view, self.sem, first(jnp.where(da == 1, 1, -1)), near)
            for step in (1, -1):
                self.go(second(step), near)

        def step_far(self):
            cond = (db == 0) & (da == 2)
            arrived(self.full, self.sem, cond)
            for step in (1, -1):
                self.go(second(step), cond)

        def step_side(self):
            arrived(self.full, self.sem, side)
            view = self.halves(jnp.where(db == 1, 0, 1))
            send(view, view, self.sem, second(jnp.where(db == 1, 1, -1)), side)

        def step_last(self):
            arrived(self.full, self.sem, db == 2)

    coarse_item = Item(seed, lambda h: seed.at[pl.ds(4 * h, 4)], seed_sem)
    fine_item = Item(
        restart.at[part], lambda h: restart.at[pl.ds(2 + 2 * c + h, 1)], restart_sem.at[0]
    )

    def seed_ready():
        arrived(seed.at[pl.ds(0, 6)], seed_sem, is_last)
        arrived(seed, seed_sem, mine == 30)

    coarse_item.root(seed_ready)

    for field, low, high, width, index in (
        (prev, prev_lo, prev_hi, 2, 0),
        (source, source_lo, source_hi, 1, 2),
        (rate, rate_lo, rate_hi, 1, 4),
    ):
        send(
            field.at[pl.ds(4 - width, width)], low, halo_sem.at[index], (y, x, c, turned(z + 1)),
            z < 3,
        )
        send(
            field.at[pl.ds(0, width)], high, halo_sem.at[index + 1], (y, x, c, turned(z - 1)),
            z > 0,
        )

    def chunk(da, db):
        return buf.at[slot(da, db)], slot_sem.at[slot(da, db)]

    def across_chip(da, db):
        view = buf.at[slot(da, db), :, pl.ds(16 * (1 - c), 48), :]
        send(view, view, slot_sem.at[slot(da, db)], partner)

    def onward(da, db):
        full, sem = chunk(da, db)
        for step in (1, -1):
            send(full, full, sem, second(step))
        across_chip(da, db)

    def relay(da, db, device, h):
        full, sem = chunk(da, db)
        arrived(full, sem)
        view = buf.at[slot(da, db), pl.ds(4 * h, 4)]
        send(view, view, sem, device)

    full, sem = chunk(0, 0)
    arrived(full.at[pl.ds(0, 6)], sem)
    for step in (1, -1):
        send(full, full, sem, first(step))
    onward(0, 0)
    fine_item.root(lambda: arrived(restart.at[part], restart_sem.at[0], mine == 30))
    relay(-1, 0, first(1), 0)
    onward(-1, 0)
    relay(1, 0, first(-1), 1)
    onward(1, 0)
    coarse_item.step_near()
    for step, h in ((-1, 0), (1, 1)):
        relay(0, step, second(-step), h)
        across_chip(0, step)
    arrived(*chunk(2, 0))
    onward(2, 0)
    coarse_item.step_far()
    fine_item.step_near()
    for a in (-1, 1):
        for step, h in ((-1, 0), (1, 1)):
            relay(a, step, second(-step), h)
            across_chip(a, step)
    arrived(*chunk(0, 2))
    across_chip(0, 2)
    coarse_item.step_side()
    for step, h in ((-1, 0), (1, 1)):
        relay(2, step, second(-step), h)
        across_chip(2, step)
    fine_item.step_far()
    for a in (-1, 1, 2):
        arrived(*chunk(a, 2))
        across_chip(a, 2)
    coarse_item.step_last()
    for a in range(4):
        for b in range(4):
            other = (a * 4 + b) * 2 + 1 - c
            arrived(buf.at[other, :, rows, :], slot_sem.at[other])
    arrived(rate_c.at[pl.ds(0, 6)], rate_sem)
    fine_item.step_side()

    state_a[...] = jnp.zeros_like(state_a)
    state_b[...] = jnp.zeros_like(state_b)
    state_a[pl.ds(1, 8), pl.ds(8, 48), :] = seed[...]
    inner = pl.ds(24, 16)
    up = (y, x, 1 - c, turned(z + c))
    down = (y, x, 1 - c, turned(z - 1 + c))

    def run(block, low, count, tiles):
        def body(i, carry):
            t = block * 8 + low + i

            def keep(ref, index):
                @pl.when(t >= 2 * chip)
                def _():
                    found[t - 2 * chip, index] = ref[:, inner, :]

            keep(state_a, 0)
            coarse_stage(state_a, state_b, rate_c, buf.at[t], 16 * c, tiles)
            keep(state_b, 1)
            coarse_stage(state_b, state_a, rate_c, buf.at[t], 16 * c, tiles)
            keep(state_a, 2)
            return carry

        lax.fori_loop(0, count, body, 0)

    for block in range(4):
        active = y >= block
        if block:
            e = block - 1

            def fill(e=e):
                edge_out[e] = state_a[pl.ds(1, 8), inner, :]

            pl.when(active)(fill)
            send(edge_out.at[e], edge_in.at[e, 0], edge_sem.at[e, 0], up, active)
            send(edge_out.at[e], edge_in.at[e, 1], edge_sem.at[e, 1], down, active)
            arrived(edge_in.at[e, 0], edge_sem.at[e, 0], active)
            arrived(edge_in.at[e, 1], edge_sem.at[e, 1], active)

            def spill(e=e):
                state_a[pl.ds(1, 8), pl.ds(8, 16), :] = edge_in[e, 0]
                state_a[pl.ds(1, 8), pl.ds(40, 16), :] = edge_in[e, 1]

            pl.when(active)(spill)
        count = jnp.where(y > block, 8, jnp.where(active, 2 * x + 2, 0))
        run(block, 0, jnp.minimum(count, 4), range(6))
        run(block, 4, jnp.maximum(count - 4, 0), range(1, 5))
        if block == 0:
            fine_item.step_last()
            own_part = restart.at[part]
            send(own_part, own_part, restart_sem.at[1], partner, mine != 30)
            send(
                restart.at[pl.ds(2, 2)], restart.at[pl.ds(6, 2)], restart_sem.at[2],
                (y, x, c, turned(z - 1)), (c == 0) & (z > 0),
            )
            send(
                restart.at[pl.ds(4, 2)], restart.at[pl.ds(0, 2)], restart_sem.at[2],
                (y, x, c, turned(z + 1)), (c == 1) & (z < 3),
            )

    for core in (0, 1):
        for d in (1, 3, 2, 0):
            to = turned(z + d)
            here = pl.ds(16 * slab, 16)
            send(
                found.at[core, :, pl.ds(2 * to, 4)], states.at[:, :, here, :], state_sem,
                (y, x, core, to), None if d else (c != core),
            )
    states[:, :, pl.ds(16 * slab, 16), :] = found[c, :, pl.ds(2 * z, 4)]

    halo_ready = ((c == 0) & (z < 3)) | ((c == 1) & (z > 0))
    halo = restart.at[pl.ds(6 - 6 * c, 2)]
    arrived(halo, restart_sem.at[2], halo_ready)
    send(halo, halo, restart_sem.at[3], partner, halo_ready)
    other_halo = ((c == 1) & (z < 3)) | ((c == 0) & (z > 0))
    arrived(restart.at[pl.ds(6 * c, 2)], restart_sem.at[3], other_halo)
    arrived(restart.at[pl.ds(4 - 2 * c, 2)], restart_sem.at[1], mine != 31)
    for index, view in enumerate((prev_lo, prev_hi, source_lo, source_hi, rate_lo, rate_hi)):
        arrived(view, halo_sem.at[index], (z > 0) if index % 2 == 0 else (z < 3))
    arrived(states.at[:, :, pl.ds(0, 112), :], state_sem)
    for cond, wait in waits:
        guarded(cond, wait)


def fine_kernel(
    prev, prev_lo, prev_hi, source, source_lo, source_hi, rate, rate_lo, rate_hi, restart, states,
    out,
    half, lifted, mixed, base, extra, last, later,
):
    z = lax.axis_index("space")
    w = stencil_weights(1.0)
    pair = pair_table(256, 128)
    spread = (
        lax.broadcasted_iota(jnp.int32, (128, 256), 0)
        == lax.broadcasted_iota(jnp.int32, (128, 256), 1) // 2
    ).astype(F32)

    def prev_layer(k):
        return prev_lo.at[k] if k < 2 else prev_hi.at[k - 6] if k > 5 else prev.at[k - 2]

    def of(low, middle, high, k):
        return low.at[0] if k < 2 else high.at[0] if k > 5 else middle.at[k - 2]

    def inside(k):
        return (z > 0) if k < 2 else (z < 3) if k > 5 else None

    def masked(k, value):
        cond = inside(k)
        return value if cond is None else jnp.where(cond, value, 0.0)

    for k in range(4):
        seed_c = 0.125 * pooled(restart[2 * k] + restart[2 * k + 1], pair, half)
        warm_c = 0.125 * pooled(
            prev_layer(2 * k)[...] + prev_layer(2 * k + 1)[...], pair, half
        )
        for n in range(3):
            change = states[n, k] - (warm_c if n else seed_c)
            wide = jnp.dot(
                change, spread, precision=lax.Precision.HIGHEST, preferred_element_type=F32
            )
            for h in range(2):
                column = wide[:, 128 * h : 128 * h + 128]
                lifted[n, k, h, pl.ds(0, 128, stride=2), :] = column
                lifted[n, k, h, pl.ds(1, 128, stride=2), :] = column

    def share(v):
        return v * pl.reciprocal(1.0 + v * v)

    def put(ref, k, i, value):
        ref[k, pl.ds(8 + 8 * i, 8), :] = value

    def guesses(i, carry):
        r = pl.ds(8 * i, 8)
        for k in range(8):
            lift = [
                jnp.concatenate([lifted[n, k // 2, h, r, :] for h in range(2)], axis=-1)
                for n in range(3)
            ]
            warm = prev_layer(k)[r, :]
            g = [masked(k, v) for v in (restart[k, r, :] + lift[0], warm + lift[1], warm + lift[2])]
            put(mixed, k, i, weights_one[0] * g[0] + weights_one[1] * g[1] + weights_one[2] * g[2])
            if 1 <= k <= 6:
                s = [share(v) for v in g]
                c = of(rate_lo, rate, rate_hi, k)[r, :]
                q = 0.5 * of(source_lo, source, source_hi, k)[r, :]
                base[k - 1, r, :] = (
                    g[0]
                    + c * (weights_one[0] * s[0] + weights_one[1] * s[1] + weights_one[2] * s[2])
                    + q
                )
                extra[k - 1, r, :] = (
                    weights_two[0] * g[0] + (weights_two[1] - 0.5) * g[1] + weights_two[2] * g[2]
                )
                if 2 <= k <= 5:
                    last[k - 2, r, :] = q + c * (
                        weights_two[0] * s[0]
                        + (weights_two[1] - 0.5) * s[1]
                        + weights_two[2] * s[2]
                    )
        return carry

    def wrap(ref, count):
        for k in range(count):
            ref[k, pl.ds(0, 8), :] = ref[k, pl.ds(256, 8), :]
            ref[k, pl.ds(264, 8), :] = ref[k, pl.ds(8, 8), :]

    def linear(ref, k, i, below, here, above):
        r = 8 * i + 8
        value = w[0] * here + w[1] * above + w[2] * below
        rows = ref[k, pl.ds(r - 8, 24), :]
        value += w[3] * rows[9:17] + w[4] * rows[7:15]
        return value + w[5] * pltpu.roll(here, 255, 1) + w[6] * pltpu.roll(here, 1, 1)

    lax.fori_loop(0, 32, guesses, 0)
    wrap(mixed, 8)

    def node_one(i, carry):
        r = pl.ds(8 * i, 8)
        planes = [mixed[k, pl.ds(8 + 8 * i, 8), :] for k in range(8)]
        for k in range(6):
            value = base[k, r, :] + linear(mixed, k + 1, i, *planes[k : k + 3])
            value = masked(0, value) if k == 0 else masked(7, value) if k == 5 else value
            if 1 <= k <= 4:
                out[0, 0, k - 1, r, :] = value
            put(later, k, i, 0.5 * value + extra[k, r, :])
        return carry

    lax.fori_loop(0, 32, node_one, 0)
    wrap(later, 6)

    def node_two(i, carry):
        r = pl.ds(8 * i, 8)
        planes = [later[k, pl.ds(8 + 8 * i, 8), :] for k in range(6)]
        for k in range(4):
            one = out[0, 0, k, r, :]
            value = one + 0.5 * rate[k, r, :] * share(one) + last[k, r, :]
            out[0, 1, k, r, :] = value + linear(later, k + 1, i, *planes[k : k + 3])
        return carry

    lax.fori_loop(0, 32, node_two, 0)


def shards(previous_end, source, rate):
    prev = previous_end[0]
    own = source[0]
    any_space = pl.BlockSpec(memory_space=pl.ANY)
    vmem = pl.BlockSpec(memory_space=pltpu.VMEM)
    dma = pltpu.SemaphoreType.DMA

    def shape(*dims):
        return jax.ShapeDtypeStruct(dims, F32)

    def scratch(*dims):
        return pltpu.VMEM(dims, F32)

    states, restart, *halos = pl.pallas_call(
        chain_kernel,
        out_shape=[shape(3, 4, 128, 128), shape(8, 256, 256)]
        + [shape(2, 256, 256)] * 2
        + [shape(1, 256, 256)] * 4,
        in_specs=[any_space] * 3,
        out_specs=[vmem] + [any_space] * 7,
        scratch_shapes=[
            scratch(4, 256, 256), scratch(4, 256, 256), scratch(4, 256, 256), scratch(256, 128),
            scratch(3, 2, 160, 128), scratch(32, 8, 64, 128), scratch(8, 48, 128),
            scratch(8, 48, 128), scratch(10, 64, 128), scratch(10, 64, 128),
            scratch(3, 8, 16, 128), scratch(3, 2, 8, 16, 128), scratch(2, 3, 10, 16, 128),
            dma((3,)), dma((N_SEND,)), dma((32,)), dma, dma, dma((3, 2)), dma, dma((6,)),
            dma((4,)),
        ],
        compiler_params=pltpu.CompilerParams(
            collective_id=0, has_side_effects=True, vmem_limit_bytes=40 * 1024 * 1024
        ),
    )(prev, own, rate)
    prev_lo, prev_hi, source_lo, source_hi, rate_lo, rate_hi = halos
    return pl.pallas_call(
        fine_kernel,
        out_shape=shape(1, 2, 4, 256, 256),
        in_specs=[vmem] * 11,
        out_specs=vmem,
        scratch_shapes=[
            scratch(256, 128), scratch(3, 4, 2, 256, 128), scratch(8, 272, 256),
            scratch(6, 256, 256), scratch(6, 256, 256), scratch(4, 256, 256),
            scratch(6, 272, 256),
        ],
        compiler_params=pltpu.CompilerParams(vmem_limit_bytes=48 * 1024 * 1024),
    )(prev, prev_lo, prev_hi, own, source_lo, source_hi, rate, rate_lo, rate_hi, restart, states)


def solution(mesh):
    torus = Mesh(
        mesh.devices.reshape(4, 4, 2, mesh.shape["space"]), ("tm_0", "tm_1", "tm_2", "space")
    )
    placed = (P(TM, "space", None, None), P(TM, "space", None, None), P("space", None, None))
    return jax.shard_map(
        shards,
        mesh=torus,
        in_specs=placed,
        out_specs=P(TM, None, "space", None, None),
        check_vma=False,
    )
```

time: 599 us -> 108 us (0.18)
  the two profiles are of different devices: /device:TPU:0 before, /device:TPU:31 now
where the time goes in v1:
time: 108 us; the launch traced here: 107 us
  Pallas kernels  102 us (94%)
  local copies, waits for them, and re-layouts  5.03 us (5%)
    pallas_call x1, Pallas kernels, shards(): pl.pallas_call(chain_kernel, out_shape=[shape(3, 4, 128, 128), shape(8, 2...  87.2 us
    pallas_call x1, Pallas kernels, shards(): pl.pallas_call(fine_kernel, out_shape=shape(1, 2, 4, 256, 256), in_specs=...  15.2 us
    unnamed x14, local copies, waits for them, and re-layouts  5.03 us

profile of v1, /device:TPU:31, one launch (start us, length us, event | category | flops | bytes accessed | tf_op | source)
XLA Modules:
  0.0 107.4 jit_solution(15339370195207335810)
XLA Ops:
  0.0 0.0 copy-start
  0.0 1.2 %copy-done = f32[1,4,256,256]{3,2,1,0:T(8,128)S(1)} copy-done((f32[1,4,256,256]{3,2,1,0:T(8,128)S(1)}, f32[1,4,256,256]{3,2,1,0:T(8,128)}, u32[]{:S(2)}) %copy-start) | copy-done | bytes 1048600
  1.2 0.0 copy-start.2
  1.2 1.2 %copy-done.2 = f32[1,4,256,256]{3,2,1,0:T(8,128)S(1)} copy-done((f32[1,4,256,256]{3,2,1,0:T(8,128)S(1)}, f32[1,4,256,256]{3,2,1,0:T(8,128)}, u32[]{:S(2)}) %copy-start.2) | copy-done | bytes 1048600
  2.5 0.0 copy-start.4
  2.5 1.2 %copy-done.4 = f32[4,256,256]{2,1,0:T(8,128)S(1)} copy-done((f32[4,256,256]{2,1,0:T(8,128)S(1)}, f32[4,256,256]{2,1,0:T(8,128)}, u32[]{:S(2)}) %copy-start.4) | copy-done | bytes 1048600
  3.7 0.0 copy-start.1
  3.7 0.0 copy-start.3
  3.7 0.0 copy-start.5
  3.7 87.2 %shard_map.37 = (f32[3,4,128,128]{3,2,1,0:T(8,128)S(1)}, f32[8,256,256]{2,1,0:T(8,128)S(1)}, f32[2,256,256]{2,1,0:T(8,128)S(1)}, f32[2,256,256]{2,1,0:T(8,128)S(...) custom-call(f32[4,256,256]{2,1,0:T(8,128)S(1)} %bitcast.2, ...), custom_call_target="tpu_custom_call" | custom-call | tf_op jit(solution)/shard_map/pallas_call | solution.py:532
  90.9 0.0 copy-start.6
  90.9 1.3 %copy-done.6 = f32[8,256,256]{2,1,0:T(8,128)} copy-done((f32[8,256,256]{2,1,0:T(8,128)}, f32[8,256,256]{2,1,0:T(8,128)S(1)}, u32[]{:S(2)}) %copy-start.6) | copy-done | bytes 2097176
  92.2 0.0 copy-done.1
  92.2 0.0 copy-done.3
  92.2 0.0 copy-done.5
  92.2 15.2 %shard_map.38 = f32[1,2,4,256,256]{4,3,2,1,0:T(8,128)} custom-call(f32[4,256,256]{2,1,0:T(8,128)S(1)} %bitcast.3, f32[2,256,256]{2,1,0:T(8,128)S(1)} %get-tuple-element.13.prev_lo, f32[2,256,256]{2,1,0:T(8,128)S(1)} %get-tuple-element.14.prev_hi, f32[4,256,256]{2,1,0:T(8,128)S(1)} %bitcast.5, f32[1,256,256]{2,1,0:T(8,128)S(1)} %get-tuple-element.15.source_lo, ...), custom_call_target="tpu_custom_call" | custom-call | tf_op jit(solution)/shard_map/pallas_call | solution.py:552
Async XLA Ops:
  0.0 1.2 %copy-start = (f32[1,4,256,256]{3,2,1,0:T(8,128)S(1)}, f32[1,4,256,256]{3,2,1,0:T(8,128)}, u32[]{:S(2)}) copy-start(f32[1,4,256,256]{3,2,1,0:T(8,128)} %param.3) | copy-start | bytes 3145732
  1.2 1.2 %copy-start.2 = (f32[1,4,256,256]{3,2,1,0:T(8,128)S(1)}, f32[1,4,256,256]{3,2,1,0:T(8,128)}, u32[]{:S(2)}) copy-start(f32[1,4,256,256]{3,2,1,0:T(8,128)} %param.4) | copy-start | bytes 3145732
  2.5 1.2 %copy-start.4 = (f32[4,256,256]{2,1,0:T(8,128)S(1)}, f32[4,256,256]{2,1,0:T(8,128)}, u32[]{:S(2)}) copy-start(f32[4,256,256]{2,1,0:T(8,128)} %rate.3) | copy-start | bytes 3145732
  3.7 88.5 %copy-start.1 = (f32[1,4,256,256]{3,2,1,0:T(8,128)S(1)}, f32[1,4,256,256]{3,2,1,0:T(8,128)}, u32[]{:S(2)}) copy-start(f32[1,4,256,256]{3,2,1,0:T(8,128)} %param.3) | copy-start | bytes 3145732
  3.7 88.5 %copy-start.3 = (f32[1,4,256,256]{3,2,1,0:T(8,128)S(1)}, f32[1,4,256,256]{3,2,1,0:T(8,128)}, u32[]{:S(2)}) copy-start(f32[1,4,256,256]{3,2,1,0:T(8,128)} %param.4) | copy-start | bytes 3145732
  3.7 88.5 %copy-start.5 = (f32[4,256,256]{2,1,0:T(8,128)S(1)}, f32[4,256,256]{2,1,0:T(8,128)}, u32[]{:S(2)}) copy-start(f32[4,256,256]{2,1,0:T(8,128)} %rate.3) | copy-start | bytes 3145732
  90.9 1.3 %copy-start.6 = (f32[8,256,256]{2,1,0:T(8,128)}, f32[8,256,256]{2,1,0:T(8,128)S(1)}, u32[]{:S(2)}) copy-start(f32[8,256,256]{2,1,0:T(8,128)S(1)} %get-tuple-element.19.restart) | copy-start | bytes 6291460

commit v2 on v1

--- a/solution.py
+++ b/solution.py
@@ -57,7 +57,7 @@
             below, here = here, above
 
 
-N_SEND = 160
+N_SEND = 256
 
 
 def chain_kernel(
@@ -65,14 +65,15 @@
     states, restart, prev_lo, prev_hi, source_lo, source_hi, rate_lo, rate_hi,
     fine_s, fine_r, fine_p, half, own, buf, rate_c, seed, state_a, state_b,
     edge_out, edge_in, found,
-    load_sem, send_sem, slot_sem, seed_sem, rate_sem, edge_sem, state_sem, halo_sem, restart_sem,
+    layer,
+    load_sem, send_sem, slot_sem, fine_sem, seed_sem, rate_sem, edge_sem, state_sem, halo_sem,
+    restart_sem,
 ):
     y, x, c, z = (lax.axis_index(name) for name in AXES)
     chip = y * 4 + x
     mine = chip * 2 + c
     slab = 2 * z + c
     is_last = mine == 31
-    root_chip = chip == 15
     partner = (y, x, 1 - c, z)
     waits = []
 
@@ -122,11 +123,15 @@
     load_s.start()
     load_r.start()
     barrier = pltpu.get_barrier_semaphore()
-    peers = [first(1), first(-1), second(1), second(-1)]
+    peers = [step(d) for step in (first, second) for d in (1, -1, 2)]
     peers += [(y, x, c, turned(z + d)) for d in (1, 2, 3)]
     peers += [(y, x, 1 - c, turned(z + d)) for d in (0, 1, 2, 3)]
     for device in peers:
         pl.semaphore_signal(barrier, inc=1, device_id=device, device_id_type=MESH)
+
+    @pl.when(jnp.logical_not(is_last))
+    def _():
+        pl.semaphore_signal(barrier, inc=1, device_id=(3, 3, 1, z), device_id_type=MESH)
 
     pair = pair_table(256, 128)
 
@@ -144,22 +149,19 @@
     pl.when(is_last)(restrict_last)
     load_s.wait()
     restrict(fine_s, 0, 0.0625)
-    pl.semaphore_wait(barrier, len(peers))
+    pl.semaphore_wait(barrier, jnp.where(is_last, len(peers) + 31, len(peers)))
 
     layers = pl.ds(2 * z, 2)
     rows = pl.ds(16 * c, 48)
-
-    for d in (0, 1, 2, 3):
-        to = turned(z + d)
-        for core in (0, 1):
-            if d or not core:
-                send(
-                    own.at[2, :, pl.ds(32 * to + 16 * core, 48), :], seed.at[layers],
-                    seed_sem, (y, x, core, to), is_last,
-                )
+    along = x * (1 - c) + y * c
+    across = y * (1 - c) + x * c
+    in_line = across == 3
+    is_root = in_line & (along == 3)
+
+    send(own.at[2, 1], layer, seed_sem.at[0], partner, is_last)
 
     def seed_self():
-        seed[layers] = own[2, :, pl.ds(32 * z + 16, 48), :]
+        layer[...] = own[2, 0]
 
     pl.when(is_last)(seed_self)
 
@@ -170,6 +172,24 @@
             (y, x, c, to),
         )
     buf[mine, layers] = own[0, :, pl.ds(32 * z, 64), :]
+    arrived(layer, seed_sem.at[0], mine == 30)
+    for d in (2, 1, -1):
+        send(layer, layer, seed_sem.at[0], first(d), is_root)
+
+    for n in range(31):
+        send(
+            fine_p.at[:, pl.ds(8 * n, 8), :], restart.at[pl.ds(2, 4), n // 2, n % 2],
+            fine_sem.at[n], (n // 8, n // 2 % 4, n % 2, z), is_last,
+        )
+
+    @pl.when(is_last)
+    def _():
+        local = pltpu.make_async_copy(
+            fine_p.at[:, pl.ds(248, 8), :], restart.at[pl.ds(2, 4), 15, 1], load_sem.at[0]
+        )
+        local.start()
+        local.wait()
+
     load_r.wait()
     restrict(fine_r, 1, 0.0625)
     for d in (1, 3, 2):
@@ -179,67 +199,20 @@
             (y, x, c, to),
         )
     rate_c[layers] = own[1, :, pl.ds(32 * z + 16 * c, 48), :]
-
-    part = pl.ds(2 + 2 * c, 2)
-    local = pltpu.make_async_copy(fine_p, restart.at[pl.ds(2, 4)], load_sem.at[0])
-
-    def place_last():
-        local.start()
-        local.wait()
-
-    send(fine_p.at[pl.ds(0, 2)], restart.at[pl.ds(2, 2)], restart_sem.at[0], partner, is_last)
-    pl.when(is_last)(place_last)
-
-    along = x * (1 - c) + y * c
-    across = y * (1 - c) + x * c
-    da, db = turned(along + 1), turned(across + 1)
-    near = (db == 0) & ((da == 1) | (da == 3))
-    side = (db == 1) | (db == 3)
-    is_root = (da == 0) & (db == 0)
-
-    class Item:
-        def __init__(self, full, halves, sem):
-            self.full, self.halves, self.sem = full, halves, sem
-
-        def go(self, device, cond):
-            send(self.full, self.full, self.sem, device, cond)
-
-        def root(self, ready):
-            ready()
-            for device in (first(1), first(-1), second(1), second(-1)):
-                self.go(device, is_root)
-
-        def step_near(self):
-            arrived(self.full, self.sem, near)
-            view = self.halves(jnp.where(da == 1, 0, 1))
-            send(view, view, self.sem, first(jnp.where(da == 1, 1, -1)), near)
-            for step in (1, -1):
-                self.go(second(step), near)
-
-        def step_far(self):
-            cond = (db == 0) & (da == 2)
-            arrived(self.full, self.sem, cond)
-            for step in (1, -1):
-                self.go(second(step), cond)
-
-        def step_side(self):
-            arrived(self.full, self.sem, side)
-            view = self.halves(jnp.where(db == 1, 0, 1))
-            send(view, view, self.sem, second(jnp.where(db == 1, 1, -1)), side)
-
-        def step_last(self):
-            arrived(self.full, self.sem, db == 2)
-
-    coarse_item = Item(seed, lambda h: seed.at[pl.ds(4 * h, 4)], seed_sem)
-    fine_item = Item(
-        restart.at[part], lambda h: restart.at[pl.ds(2 + 2 * c + h, 1)], restart_sem.at[0]
-    )
-
-    def seed_ready():
-        arrived(seed.at[pl.ds(0, 6)], seed_sem, is_last)
-        arrived(seed, seed_sem, mine == 30)
-
-    coarse_item.root(seed_ready)
+    arrived(layer, seed_sem.at[0], in_line & (along != 3))
+    for d in (2, 1, -1):
+        send(layer, layer, seed_sem.at[0], second(d), in_line)
+
+    def spread_seed():
+        arrived(layer, seed_sem.at[0], jnp.logical_not(in_line))
+        target = 2 * z + 1 - c
+        for d in (1, 3, 2, 0):
+            for core in (0, 1):
+                to = turned(z + d)
+                view = layer.at[pl.ds(32 * to + 16 * core, 48), :]
+                cond = None if d else (c != core)
+                send(view, seed.at[target], seed_sem.at[1], (y, x, core, to), cond)
+        seed[target] = layer[pl.ds(32 * z + 16 * c, 48), :]
 
     for field, low, high, width, index in (
         (prev, prev_lo, prev_hi, 2, 0),
@@ -274,45 +247,72 @@
         view = buf.at[slot(da, db), pl.ds(4 * h, 4)]
         send(view, view, sem, device)
 
+    def fine(da, db):
+        here = slot(da, db)
+        return restart.at[pl.ds(2, 4), here // 2, c], fine_sem.at[here]
+
+    def fine_onward(da, db):
+        full, sem = fine(da, db)
+        for step in (1, -1):
+            send(full, full, sem, second(step))
+
+    def fine_relay(da, db, device, h):
+        full, sem = fine(da, db)
+        arrived(full, sem)
+        view = restart.at[pl.ds(2 + 2 * h, 2), slot(da, db) // 2, c]
+        send(view, view, sem, device)
+
+    def fine_own():
+        full, sem = fine(0, 0)
+        arrived(full, sem, jnp.logical_not(is_last))
+        for step in (1, -1):
+            send(full, full, sem, first(step))
+        fine_onward(0, 0)
+
+    def near(relay, onward):
+        relay(-1, 0, first(1), 0)
+        onward(-1, 0)
+        relay(1, 0, first(-1), 1)
+        onward(1, 0)
+
+    def ring(relay, a):
+        for step, h in ((-1, 0), (1, 1)):
+            relay(a, step, second(-step), h)
+            if relay is not fine_relay:
+                across_chip(a, step)
+
     full, sem = chunk(0, 0)
     arrived(full.at[pl.ds(0, 6)], sem)
     for step in (1, -1):
         send(full, full, sem, first(step))
     onward(0, 0)
-    fine_item.root(lambda: arrived(restart.at[part], restart_sem.at[0], mine == 30))
-    relay(-1, 0, first(1), 0)
-    onward(-1, 0)
-    relay(1, 0, first(-1), 1)
-    onward(1, 0)
-    coarse_item.step_near()
-    for step, h in ((-1, 0), (1, 1)):
-        relay(0, step, second(-step), h)
-        across_chip(0, step)
+    fine_own()
+    near(relay, onward)
+    spread_seed()
+    ring(relay, 0)
+    near(fine_relay, fine_onward)
     arrived(*chunk(2, 0))
     onward(2, 0)
-    coarse_item.step_far()
-    fine_item.step_near()
-    for a in (-1, 1):
-        for step, h in ((-1, 0), (1, 1)):
-            relay(a, step, second(-step), h)
-            across_chip(a, step)
+    ring(relay, -1)
+    ring(relay, 1)
+    ring(fine_relay, 0)
+    arrived(*fine(2, 0))
+    fine_onward(2, 0)
     arrived(*chunk(0, 2))
     across_chip(0, 2)
-    coarse_item.step_side()
-    for step, h in ((-1, 0), (1, 1)):
-        relay(2, step, second(-step), h)
-        across_chip(2, step)
-    fine_item.step_far()
+    ring(relay, 2)
+    ring(fine_relay, -1)
+    ring(fine_relay, 1)
     for a in (-1, 1, 2):
         arrived(*chunk(a, 2))
         across_chip(a, 2)
-    coarse_item.step_last()
+    ring(fine_relay, 2)
     for a in range(4):
         for b in range(4):
             other = (a * 4 + b) * 2 + 1 - c
             arrived(buf.at[other, :, rows, :], slot_sem.at[other])
     arrived(rate_c.at[pl.ds(0, 6)], rate_sem)
-    fine_item.step_side()
+    arrived(seed.at[pl.ds(0, 7)], seed_sem.at[1])
 
     state_a[...] = jnp.zeros_like(state_a)
     state_b[...] = jnp.zeros_like(state_b)
@@ -362,17 +362,16 @@
         run(block, 0, jnp.minimum(count, 4), range(6))
         run(block, 4, jnp.maximum(count - 4, 0), range(1, 5))
         if block == 0:
-            fine_item.step_last()
-            own_part = restart.at[part]
-            send(own_part, own_part, restart_sem.at[1], partner, mine != 30)
-            send(
-                restart.at[pl.ds(2, 2)], restart.at[pl.ds(6, 2)], restart_sem.at[2],
-                (y, x, c, turned(z - 1)), (c == 0) & (z > 0),
-            )
-            send(
-                restart.at[pl.ds(4, 2)], restart.at[pl.ds(0, 2)], restart_sem.at[2],
-                (y, x, c, turned(z + 1)), (c == 1) & (z < 3),
-            )
+            for a in (0, -1, 1, 2):
+                arrived(*fine(a, 2))
+            view = restart.at[pl.ds(2, 4), :, c]
+            send(view, view, restart_sem.at[0], partner)
+            for low, to, step, index in ((2, 6, -1, 1), (4, 0, 1, 2)):
+                send(
+                    restart.at[pl.ds(low, 2), :, c], restart.at[pl.ds(to, 2), :, c],
+                    restart_sem.at[index], (y, x, c, turned(z + step)),
+                    (z > 0) if step < 0 else (z < 3),
+                )
 
     for core in (0, 1):
         for d in (1, 3, 2, 0):
@@ -384,13 +383,13 @@
             )
     states[:, :, pl.ds(16 * slab, 16), :] = found[c, :, pl.ds(2 * z, 4)]
 
-    halo_ready = ((c == 0) & (z < 3)) | ((c == 1) & (z > 0))
-    halo = restart.at[pl.ds(6 - 6 * c, 2)]
-    arrived(halo, restart_sem.at[2], halo_ready)
-    send(halo, halo, restart_sem.at[3], partner, halo_ready)
-    other_halo = ((c == 1) & (z < 3)) | ((c == 0) & (z > 0))
-    arrived(restart.at[pl.ds(6 * c, 2)], restart_sem.at[3], other_halo)
-    arrived(restart.at[pl.ds(4 - 2 * c, 2)], restart_sem.at[1], mine != 31)
+    for low, index, cond in ((6, 1, z < 3), (0, 2, z > 0)):
+        view = restart.at[pl.ds(low, 2), :, c]
+        arrived(view, restart_sem.at[index], cond)
+        send(view, view, restart_sem.at[index + 2], partner, cond)
+    for low, index, cond in ((6, 3, z < 3), (0, 4, z > 0)):
+        arrived(restart.at[pl.ds(low, 2), :, 1 - c], restart_sem.at[index], cond)
+    arrived(restart.at[pl.ds(2, 4), :, 1 - c], restart_sem.at[0])
     for index, view in enumerate((prev_lo, prev_hi, source_lo, source_hi, rate_lo, rate_hi)):
         arrived(view, halo_sem.at[index], (z > 0) if index % 2 == 0 else (z < 3))
     arrived(states.at[:, :, pl.ds(0, 112), :], state_sem)
@@ -398,11 +397,16 @@
         guarded(cond, wait)
 
 
-def fine_kernel(
-    prev, prev_lo, prev_hi, source, source_lo, source_hi, rate, rate_lo, rate_hi, restart, states,
-    out,
-    half, lifted, mixed, base, extra, last, later,
-):
+def fine_kernel(*refs):
+    inputs, out = refs[:11], refs[11]
+    half, lifted, mixed, base, extra, last, later = refs[12:19]
+    held, load_sem = refs[19:30], refs[30]
+    loads = [
+        pltpu.make_async_copy(a, b, load_sem.at[n]) for n, (a, b) in enumerate(zip(inputs, held))
+    ]
+    for n in (10, 9, 0, 1, 2, 3, 4, 5, 6, 7, 8):
+        loads[n].start()
+    prev, prev_lo, prev_hi, source, source_lo, source_hi, rate, rate_lo, rate_hi, restart, states = held
     z = lax.axis_index("space")
     w = stencil_weights(1.0)
     pair = pair_table(256, 128)
@@ -424,6 +428,8 @@
         cond = inside(k)
         return value if cond is None else jnp.where(cond, value, 0.0)
 
+    for n in (10, 9, 0, 1, 2):
+        loads[n].wait()
     for k in range(4):
         seed_c = 0.125 * pooled(restart[2 * k] + restart[2 * k + 1], pair, half)
         warm_c = 0.125 * pooled(
@@ -443,7 +449,11 @@
         return v * pl.reciprocal(1.0 + v * v)
 
     def put(ref, k, i, value):
-        ref[k, pl.ds(8 + 8 * i, 8), :] = value
+        for h in range(2):
+            ref[k, h, pl.ds(8 + 8 * i, 8), :] = value[:, 128 * h : 128 * h + 128]
+
+    def row(ref, k, start):
+        return jnp.concatenate([ref[k, h, pl.ds(start, 8), :] for h in range(2)], axis=-1)
 
     def guesses(i, carry):
         r = pl.ds(8 * i, 8)
@@ -477,22 +487,24 @@
 
     def wrap(ref, count):
         for k in range(count):
-            ref[k, pl.ds(0, 8), :] = ref[k, pl.ds(256, 8), :]
-            ref[k, pl.ds(264, 8), :] = ref[k, pl.ds(8, 8), :]
+            for h in range(2):
+                ref[k, h, pl.ds(0, 8), :] = ref[k, h, pl.ds(256, 8), :]
+                ref[k, h, pl.ds(264, 8), :] = ref[k, h, pl.ds(8, 8), :]
 
     def linear(ref, k, i, below, here, above):
         r = 8 * i + 8
         value = w[0] * here + w[1] * above + w[2] * below
-        rows = ref[k, pl.ds(r - 8, 24), :]
-        value += w[3] * rows[9:17] + w[4] * rows[7:15]
+        value += w[3] * row(ref, k, r + 1) + w[4] * row(ref, k, r - 1)
         return value + w[5] * pltpu.roll(here, 255, 1) + w[6] * pltpu.roll(here, 1, 1)
 
-    lax.fori_loop(0, 32, guesses, 0)
+    for n in range(3, 9):
+        loads[n].wait()
+    lax.fori_loop(0, 32, guesses, 0, unroll=2)
     wrap(mixed, 8)
 
     def node_one(i, carry):
         r = pl.ds(8 * i, 8)
-        planes = [mixed[k, pl.ds(8 + 8 * i, 8), :] for k in range(8)]
+        planes = [row(mixed, k, 8 + 8 * i) for k in range(8)]
         for k in range(6):
             value = base[k, r, :] + linear(mixed, k + 1, i, *planes[k : k + 3])
             value = masked(0, value) if k == 0 else masked(7, value) if k == 5 else value
@@ -501,19 +513,19 @@
             put(later, k, i, 0.5 * value + extra[k, r, :])
         return carry
 
-    lax.fori_loop(0, 32, node_one, 0)
+    lax.fori_loop(0, 32, node_one, 0, unroll=4)
     wrap(later, 6)
 
     def node_two(i, carry):
         r = pl.ds(8 * i, 8)
-        planes = [later[k, pl.ds(8 + 8 * i, 8), :] for k in range(6)]
+        planes = [row(later, k, 8 + 8 * i) for k in range(6)]
         for k in range(4):
             one = out[0, 0, k, r, :]
             value = one + 0.5 * rate[k, r, :] * share(one) + last[k, r, :]
             out[0, 1, k, r, :] = value + linear(later, k + 1, i, *planes[k : k + 3])
         return carry
 
-    lax.fori_loop(0, 32, node_two, 0)
+    lax.fori_loop(0, 32, node_two, 0, unroll=4)
 
 
 def shards(previous_end, source, rate):
@@ -531,7 +543,7 @@
 
     states, restart, *halos = pl.pallas_call(
         chain_kernel,
-        out_shape=[shape(3, 4, 128, 128), shape(8, 256, 256)]
+        out_shape=[shape(3, 4, 128, 128), shape(8, 16, 2, 8, 256)]
         + [shape(2, 256, 256)] * 2
         + [shape(1, 256, 256)] * 4,
         in_specs=[any_space] * 3,
@@ -541,25 +553,31 @@
             scratch(3, 2, 160, 128), scratch(32, 8, 64, 128), scratch(8, 48, 128),
             scratch(8, 48, 128), scratch(10, 64, 128), scratch(10, 64, 128),
             scratch(3, 8, 16, 128), scratch(3, 2, 8, 16, 128), scratch(2, 3, 10, 16, 128),
-            dma((3,)), dma((N_SEND,)), dma((32,)), dma, dma, dma((3, 2)), dma, dma((6,)),
-            dma((4,)),
+            scratch(160, 128),
+            dma((3,)), dma((N_SEND,)), dma((32,)), dma((32,)), dma((2,)), dma, dma((3, 2)), dma,
+            dma((6,)), dma((5,)),
         ],
         compiler_params=pltpu.CompilerParams(
-            collective_id=0, has_side_effects=True, vmem_limit_bytes=40 * 1024 * 1024
+            collective_id=0, has_side_effects=True, vmem_limit_bytes=63 * 1024 * 1024
         ),
     )(prev, own, rate)
     prev_lo, prev_hi, source_lo, source_hi, rate_lo, rate_hi = halos
+    restart = restart.reshape(8, 256, 256)
     return pl.pallas_call(
         fine_kernel,
         out_shape=shape(1, 2, 4, 256, 256),
-        in_specs=[vmem] * 11,
+        in_specs=[any_space] * 11,
         out_specs=vmem,
         scratch_shapes=[
-            scratch(256, 128), scratch(3, 4, 2, 256, 128), scratch(8, 272, 256),
+            scratch(256, 128), scratch(3, 4, 2, 256, 128), scratch(8, 2, 272, 128),
             scratch(6, 256, 256), scratch(6, 256, 256), scratch(4, 256, 256),
-            scratch(6, 272, 256),
+            scratch(6, 2, 272, 128),
+            scratch(4, 256, 256), scratch(2, 256, 256), scratch(2, 256, 256),
+            scratch(4, 256, 256), scratch(1, 256, 256), scratch(1, 256, 256),
+            scratch(4, 256, 256), scratch(1, 256, 256), scratch(1, 256, 256),
+            scratch(8, 256, 256), scratch(3, 4, 128, 128), dma((11,)),
         ],
-        compiler_params=pltpu.CompilerParams(vmem_limit_bytes=48 * 1024 * 1024),
+        compiler_params=pltpu.CompilerParams(vmem_limit_bytes=63 * 1024 * 1024),
     )(prev, prev_lo, prev_hi, own, source_lo, source_hi, rate, rate_lo, rate_hi, restart, states)
 
 

time: 108 us -> 91 us (0.84)
  the two profiles are of different devices: /device:TPU:31 before, /device:TPU:29 now
where the time goes in v2:
time: 91 us; the launch traced here: 90.9 us
  Pallas kernels  90.9 us (100%)
    pallas_call x1, Pallas kernels, shards(): pl.pallas_call(chain_kernel, out_shape=[shape(3, 4, 128, 128), shape(8, 1...  78.4 us
    pallas_call x1, Pallas kernels, shards(): pl.pallas_call(fine_kernel, out_shape=shape(1, 2, 4, 256, 256), in_specs=...  12.5 us

profile of v2, /device:TPU:29, one launch (start us, length us, event | category | flops | bytes accessed | tf_op | source)
XLA Modules:
  0.0 90.9 jit_solution(18182148170006573402)
XLA Ops:
  0.0 78.4 %shard_map.37 = (f32[3,4,128,128]{3,2,1,0:T(8,128)}, f32[8,16,2,8,256]{4,3,2,1,0:T(8,128)}, f32[2,256,256]{2,1,0:T(8,128)}, f32[2,256,256]{2,1,0:T(8,128)}, f32[...) custom-call(f32[4,256,256]{2,1,0:T(8,128)} %bitcast.3, ...), custom_call_target="tpu_custom_call" | custom-call | tf_op jit(solution)/shard_map/pallas_call | solution.py:544
  78.4 12.5 %shard_map.38 = f32[1,2,4,256,256]{4,3,2,1,0:T(8,128)} custom-call(f32[4,256,256]{2,1,0:T(8,128)} %bitcast.4, f32[2,256,256]{2,1,0:T(8,128)} %get-tuple-element.13.refs_1_, f32[2,256,256]{2,1,0:T(8,128)} %get-tuple-element.14.refs_2_, f32[4,256,256]{2,1,0:T(8,128)} %bitcast.6, f32[1,256,256]{2,1,0:T(8,128)} %get-tuple-element.15.refs_4_, ...), custom_call_target="tpu_custom_call" | custom-call | tf_op jit(solution)/shard_map/pallas_call | solution.py:566

commit v3 on v2

--- a/solution.py
+++ b/solution.py
@@ -40,20 +40,20 @@
     return scratch[pl.ds(0, 128, stride=2), :] + scratch[pl.ds(1, 128, stride=2), :]
 
 
-def coarse_stage(src, dst, rate, source, row, tiles):
+def coarse_stage(src, dst, planes, starts, at):
     w = [0.5 * v for v in stencil_weights(2.0)]
-    for j in tiles:
-        r = 8 + 8 * j
-        below = src[0, pl.ds(r, 8), :]
-        here = src[1, pl.ds(r, 8), :]
-        for k in range(1, 9):
+    for j, r in enumerate(starts):
+        below = src[planes[0][0] - 1, pl.ds(r, 8), :]
+        here = src[planes[0][0], pl.ds(r, 8), :]
+        for k, to, n in planes:
             above = src[k + 1, pl.ds(r, 8), :]
-            out = (1.0 + w[0]) * here + source[k - 1, pl.ds(row + 8 * j, 8), :]
+            rate, source = at(n, j)
+            out = (1.0 + w[0]) * here + source
             out += w[1] * above + w[2] * below
             out += w[3] * src[k, pl.ds(r + 1, 8), :] + w[4] * src[k, pl.ds(r - 1, 8), :]
             out += w[5] * pltpu.roll(here, 127, 1) + w[6] * pltpu.roll(here, 1, 1)
-            out += rate[k - 1, pl.ds(8 * j, 8), :] * here * pl.reciprocal(1.0 + here * here)
-            dst[k, pl.ds(r, 8), :] = out
+            out += rate * here * pl.reciprocal(1.0 + here * here)
+            dst[to, pl.ds(r, 8), :] = out
             below, here = here, above
 
 
@@ -64,10 +64,9 @@
     prev, source, rate,
     states, restart, prev_lo, prev_hi, source_lo, source_hi, rate_lo, rate_hi,
     fine_s, fine_r, fine_p, half, own, buf, rate_c, seed, state_a, state_b,
-    edge_out, edge_in, found,
-    layer,
+    edge_out, edge_in, found, layer, start, mid, end_state, near_c, warm,
     load_sem, send_sem, slot_sem, fine_sem, seed_sem, rate_sem, edge_sem, state_sem, halo_sem,
-    restart_sem,
+    restart_sem, near_sem, halo_piece,
 ):
     y, x, c, z = (lax.axis_index(name) for name in AXES)
     chip = y * 4 + x
@@ -119,7 +118,7 @@
     load_p = pltpu.make_async_copy(prev, fine_p, load_sem.at[0])
     load_s = pltpu.make_async_copy(source, fine_s, load_sem.at[1])
     load_r = pltpu.make_async_copy(rate, fine_r, load_sem.at[2])
-    pl.when(is_last)(load_p.start)
+    load_p.start()
     load_s.start()
     load_r.start()
     barrier = pltpu.get_barrier_semaphore()
@@ -142,11 +141,8 @@
             own[index, k, pl.ds(0, 16), :] = total[112:128]
             own[index, k, pl.ds(144, 16), :] = total[0:16]
 
-    def restrict_last():
-        load_p.wait()
-        restrict(fine_p, 2, 0.125)
-
-    pl.when(is_last)(restrict_last)
+    load_p.wait()
+    pl.when(is_last)(lambda: restrict(fine_p, 2, 0.125))
     load_s.wait()
     restrict(fine_s, 0, 0.0625)
     pl.semaphore_wait(barrier, jnp.where(is_last, len(peers) + 31, len(peers)))
@@ -175,6 +171,28 @@
     arrived(layer, seed_sem.at[0], mine == 30)
     for d in (2, 1, -1):
         send(layer, layer, seed_sem.at[0], first(d), is_root)
+
+    def fine_halo(field, low, high, width, index):
+        send(
+            field.at[pl.ds(4 - width, width)], low, halo_sem.at[index], (y, x, c, turned(z + 1)),
+            z < 3,
+        )
+        send(
+            field.at[pl.ds(0, width)], high, halo_sem.at[index + 1], (y, x, c, turned(z - 1)),
+            z > 0,
+        )
+
+    def other_halos():
+        for f in range(2):
+            for n, step, cond in ((0, 1, z < 3), (1, -1, z > 0)):
+                send(
+                    own.at[f, :, pl.ds(16, 128), :], near_c.at[f, pl.ds(4 * n, 2)],
+                    near_sem.at[f, n], (y, x, c, turned(z + step)), cond,
+                )
+        fine_halo(source, source_lo, source_hi, 1, 2)
+        fine_halo(rate, rate_lo, rate_hi, 1, 4)
+
+    fine_halo(prev, prev_lo, prev_hi, 2, 0)
 
     for n in range(31):
         send(
@@ -214,20 +232,6 @@
                 send(view, seed.at[target], seed_sem.at[1], (y, x, core, to), cond)
         seed[target] = layer[pl.ds(32 * z + 16 * c, 48), :]
 
-    for field, low, high, width, index in (
-        (prev, prev_lo, prev_hi, 2, 0),
-        (source, source_lo, source_hi, 1, 2),
-        (rate, rate_lo, rate_hi, 1, 4),
-    ):
-        send(
-            field.at[pl.ds(4 - width, width)], low, halo_sem.at[index], (y, x, c, turned(z + 1)),
-            z < 3,
-        )
-        send(
-            field.at[pl.ds(0, width)], high, halo_sem.at[index + 1], (y, x, c, turned(z - 1)),
-            z > 0,
-        )
-
     def chunk(da, db):
         return buf.at[slot(da, db)], slot_sem.at[slot(da, db)]
 
@@ -289,6 +293,7 @@
     fine_own()
     near(relay, onward)
     spread_seed()
+    other_halos()
     ring(relay, 0)
     near(fine_relay, fine_onward)
     arrived(*chunk(2, 0))
@@ -301,12 +306,9 @@
     arrived(*chunk(0, 2))
     across_chip(0, 2)
     ring(relay, 2)
-    ring(fine_relay, -1)
-    ring(fine_relay, 1)
     for a in (-1, 1, 2):
         arrived(*chunk(a, 2))
         across_chip(a, 2)
-    ring(fine_relay, 2)
     for a in range(4):
         for b in range(4):
             other = (a * 4 + b) * 2 + 1 - c
@@ -325,16 +327,18 @@
         def body(i, carry):
             t = block * 8 + low + i
 
-            def keep(ref, index):
-                @pl.when(t >= 2 * chip)
-                def _():
-                    found[t - 2 * chip, index] = ref[:, inner, :]
-
-            keep(state_a, 0)
-            coarse_stage(state_a, state_b, rate_c, buf.at[t], 16 * c, tiles)
-            keep(state_b, 1)
-            coarse_stage(state_b, state_a, rate_c, buf.at[t], 16 * c, tiles)
-            keep(state_a, 2)
+            @pl.when(t == 2 * chip)
+            def _():
+                found[0] = state_a[pl.ds(1, 8), inner, :]
+
+            def at(n, j):
+                r = 8 * tiles[j]
+                return rate_c[n, pl.ds(r, 8), :], buf[t, n, pl.ds(16 * c + r, 8), :]
+
+            planes = [(k, k, k - 1) for k in range(1, 9)]
+            starts = [8 + 8 * tile for tile in tiles]
+            coarse_stage(state_a, state_b, planes, starts, at)
+            coarse_stage(state_b, state_a, planes, starts, at)
             return carry
 
         lax.fori_loop(0, count, body, 0)
@@ -350,6 +354,21 @@
             pl.when(active)(fill)
             send(edge_out.at[e], edge_in.at[e, 0], edge_sem.at[e, 0], up, active)
             send(edge_out.at[e], edge_in.at[e, 1], edge_sem.at[e, 1], down, active)
+            if block == 1:
+                for a in (-1, 1, 2):
+                    ring(fine_relay, a)
+                for a in (0, -1, 1, 2):
+                    arrived(*fine(a, 2))
+                view = restart.at[pl.ds(2, 4), :, c]
+                send(view, view, restart_sem.at[0], partner)
+            for piece in ((0,), (1, 2), (3,))[e]:
+                for low, to, step, index in ((2, 6, -1, 1), (4, 0, 1, 2)):
+                    some = pl.ds(4 * piece, 4)
+                    send(
+                        restart.at[pl.ds(low, 2), some, c], restart.at[pl.ds(to, 2), some, c],
+                        halo_piece.at[index - 1, piece], (y, x, c, turned(z + step)),
+                        (z > 0) if step < 0 else (z < 3),
+                    )
             arrived(edge_in.at[e, 0], edge_sem.at[e, 0], active)
             arrived(edge_in.at[e, 1], edge_sem.at[e, 1], active)
 
@@ -358,41 +377,106 @@
                 state_a[pl.ds(1, 8), pl.ds(40, 16), :] = edge_in[e, 1]
 
             pl.when(active)(spill)
-        count = jnp.where(y > block, 8, jnp.where(active, 2 * x + 2, 0))
+        count = jnp.where(y > block, 8, jnp.where(active, 2 * x + 1, 0))
         run(block, 0, jnp.minimum(count, 4), range(6))
         run(block, 4, jnp.maximum(count - 4, 0), range(1, 5))
-        if block == 0:
-            for a in (0, -1, 1, 2):
-                arrived(*fine(a, 2))
-            view = restart.at[pl.ds(2, 4), :, c]
-            send(view, view, restart_sem.at[0], partner)
-            for low, to, step, index in ((2, 6, -1, 1), (4, 0, 1, 2)):
+
+    found[1] = state_a[pl.ds(1, 8), inner, :]
+    here = pl.ds(8 + 16 * slab, 16)
+    for d in (1, 3, 2, 0):
+        to = turned(z + d)
+        end = (to == 0) | (to == 3)
+        for core in (0, 1):
+            for count, low, cond in (
+                (5, jnp.where(to == 0, 0, 3), end),
+                (7, jnp.where(to == 1, 0, 1), jnp.logical_not(end)),
+            ):
                 send(
-                    restart.at[pl.ds(low, 2), :, c], restart.at[pl.ds(to, 2), :, c],
-                    restart_sem.at[index], (y, x, c, turned(z + step)),
-                    (z > 0) if step < 0 else (z < 3),
+                    found.at[core, pl.ds(low, count)], start.at[pl.ds(3 + low, count), here, :],
+                    state_sem, (y, x, core, to), cond if d else cond & (c != core),
                 )
-
-    for core in (0, 1):
-        for d in (1, 3, 2, 0):
-            to = turned(z + d)
-            here = pl.ds(16 * slab, 16)
-            send(
-                found.at[core, :, pl.ds(2 * to, 4)], states.at[:, :, here, :], state_sem,
-                (y, x, core, to), None if d else (c != core),
-            )
-    states[:, :, pl.ds(16 * slab, 16), :] = found[c, :, pl.ds(2 * z, 4)]
+    zero = jnp.zeros((3, 144, 128), F32)
+    start[pl.ds(0, 3)] = zero
+    start[pl.ds(11, 3)] = zero
+    start[pl.ds(3, 8), here, :] = found[c]
+
+    for index in (0, 1):
+        arrived((prev_lo, prev_hi)[index], halo_sem.at[index], (z < 3) if index else (z > 0))
+    sides = [
+        pltpu.make_async_copy(view, fine_r.at[pl.ds(2 * n, 2)], load_sem.at[1 + n])
+        for n, view in enumerate((prev_lo, prev_hi))
+    ]
+    for copy in sides:
+        copy.start()
+    for n in range(2):
+        warm[1 + n] = 0.125 * pooled(fine_p[2 * n] + fine_p[2 * n + 1], pair, half)
+    for copy in sides:
+        copy.wait()
+    for n in range(2):
+        warm[3 * n] = 0.125 * pooled(fine_r[2 * n] + fine_r[2 * n + 1], pair, half)
+    for f in range(2):
+        near_c[f, pl.ds(2, 2)] = own[f, :, pl.ds(16, 128), :]
+        for n, cond in ((0, z > 0), (1, z < 3)):
+            arrived(near_c.at[f, pl.ds(4 * n, 2)], near_sem.at[f, n], cond)
+    for count, cond in ((5, (z == 0) | (z == 3)), (7, (z == 1) | (z == 2))):
+        arrived(start.at[pl.ds(0, count), pl.ds(0, 112), :], state_sem, cond)
+
+    first_low = 2 * z + 1
+
+    def wrapped(ref, low, count):
+        for k in range(count):
+            ref[low + k, pl.ds(0, 8), :] = ref[low + k, pl.ds(128, 8), :]
+            ref[low + k, pl.ds(136, 8), :] = ref[low + k, pl.ds(8, 8), :]
+
+    wrapped(start, 2 * z, 8)
+
+    def rows_of(i):
+        def at(n, j):
+            r = pl.ds(16 * i + 8 * j, 8)
+            return near_c[1, n, r, :], near_c[0, n, r, :]
+
+        return [8 + 16 * i, 16 + 16 * i], at
+
+    def half_one(i, carry):
+        starts, at = rows_of(i)
+        planes = [(first_low + n, n, n) for n in range(6)]
+        coarse_stage(start, mid, planes, starts, at)
+        return carry
+
+    lax.fori_loop(0, 8, half_one, 0, unroll=2)
+
+    @pl.when(z == 0)
+    def _():
+        mid[pl.ds(0, 2)] = jnp.zeros((2, 144, 128), F32)
+
+    @pl.when(z == 3)
+    def _():
+        mid[pl.ds(4, 2)] = jnp.zeros((2, 144, 128), F32)
+
+    wrapped(mid, 0, 6)
+
+    def half_two(i, carry):
+        starts, at = rows_of(i)
+        planes = [(n + 1, n, n + 1) for n in range(4)]
+        coarse_stage(mid, end_state, planes, starts, at)
+        return carry
+
+    lax.fori_loop(0, 8, half_two, 0, unroll=2)
+    states[0] = start[pl.ds(2 * z + 2, 4), pl.ds(8, 128), :]
+    states[1] = mid[pl.ds(1, 4), pl.ds(8, 128), :] - warm[...]
+    states[2] = end_state[:, pl.ds(8, 128), :] - warm[...]
 
     for low, index, cond in ((6, 1, z < 3), (0, 2, z > 0)):
+        for piece in range(4):
+            view = restart.at[pl.ds(low, 2), pl.ds(4 * piece, 4), c]
+            arrived(view, halo_piece.at[index - 1, piece], cond)
         view = restart.at[pl.ds(low, 2), :, c]
-        arrived(view, restart_sem.at[index], cond)
         send(view, view, restart_sem.at[index + 2], partner, cond)
     for low, index, cond in ((6, 3, z < 3), (0, 4, z > 0)):
         arrived(restart.at[pl.ds(low, 2), :, 1 - c], restart_sem.at[index], cond)
     arrived(restart.at[pl.ds(2, 4), :, 1 - c], restart_sem.at[0])
-    for index, view in enumerate((prev_lo, prev_hi, source_lo, source_hi, rate_lo, rate_hi)):
-        arrived(view, halo_sem.at[index], (z > 0) if index % 2 == 0 else (z < 3))
-    arrived(states.at[:, :, pl.ds(0, 112), :], state_sem)
+    for index, view in enumerate((source_lo, source_hi, rate_lo, rate_hi)):
+        arrived(view, halo_sem.at[index + 2], (z > 0) if index % 2 == 0 else (z < 3))
     for cond, wait in waits:
         guarded(cond, wait)
 
@@ -428,15 +512,12 @@
         cond = inside(k)
         return value if cond is None else jnp.where(cond, value, 0.0)
 
-    for n in (10, 9, 0, 1, 2):
-        loads[n].wait()
+    loads[10].wait()
+    loads[9].wait()
     for k in range(4):
         seed_c = 0.125 * pooled(restart[2 * k] + restart[2 * k + 1], pair, half)
-        warm_c = 0.125 * pooled(
-            prev_layer(2 * k)[...] + prev_layer(2 * k + 1)[...], pair, half
-        )
         for n in range(3):
-            change = states[n, k] - (warm_c if n else seed_c)
+            change = states[n, k] if n else states[n, k] - seed_c
             wide = jnp.dot(
                 change, spread, precision=lax.Precision.HIGHEST, preferred_element_type=F32
             )
@@ -497,7 +578,7 @@
         value += w[3] * row(ref, k, r + 1) + w[4] * row(ref, k, r - 1)
         return value + w[5] * pltpu.roll(here, 255, 1) + w[6] * pltpu.roll(here, 1, 1)
 
-    for n in range(3, 9):
+    for n in range(9):
         loads[n].wait()
     lax.fori_loop(0, 32, guesses, 0, unroll=2)
     wrap(mixed, 8)
@@ -552,10 +633,11 @@
             scratch(4, 256, 256), scratch(4, 256, 256), scratch(4, 256, 256), scratch(256, 128),
             scratch(3, 2, 160, 128), scratch(32, 8, 64, 128), scratch(8, 48, 128),
             scratch(8, 48, 128), scratch(10, 64, 128), scratch(10, 64, 128),
-            scratch(3, 8, 16, 128), scratch(3, 2, 8, 16, 128), scratch(2, 3, 10, 16, 128),
-            scratch(160, 128),
+            scratch(3, 8, 16, 128), scratch(3, 2, 8, 16, 128), scratch(2, 8, 16, 128),
+            scratch(160, 128), scratch(14, 144, 128), scratch(6, 144, 128), scratch(4, 144, 128),
+            scratch(2, 6, 128, 128), scratch(4, 128, 128),
             dma((3,)), dma((N_SEND,)), dma((32,)), dma((32,)), dma((2,)), dma, dma((3, 2)), dma,
-            dma((6,)), dma((5,)),
+            dma((6,)), dma((5,)), dma((2, 2)), dma((2, 4)),
         ],
         compiler_params=pltpu.CompilerParams(
             collective_id=0, has_side_effects=True, vmem_limit_bytes=63 * 1024 * 1024

time: 91 us -> 81.8 us (0.90)
  Pallas kernels: 90.9 us -> 81.2 us
    pallas_call x1, Pallas kernels: 78.4 us -> 69.3 us  [shards(): pl.pallas_call(chain_kernel, out_shape=[shape(3, 4, 128, 128), shape(8, 1...]
where the time goes in v3:
time: 81.8 us; the launch traced here: 81.2 us
  Pallas kernels  81.2 us (99%)
    pallas_call x1, Pallas kernels, shards(): pl.pallas_call(chain_kernel, out_shape=[shape(3, 4, 128, 128), shape(8, 1...  69.3 us
    pallas_call x1, Pallas kernels, shards(): pl.pallas_call(fine_kernel, out_shape=shape(1, 2, 4, 256, 256), in_specs=...  11.9 us

profile of v3, /device:TPU:29, one launch (start us, length us, event | category | flops | bytes accessed | tf_op | source)
XLA Modules:
  0.0 81.2 jit_solution(6501484994584348875)
XLA Ops:
  0.0 69.3 %shard_map.37 = (f32[3,4,128,128]{3,2,1,0:T(8,128)}, f32[8,16,2,8,256]{4,3,2,1,0:T(8,128)}, f32[2,256,256]{2,1,0:T(8,128)}, f32[2,256,256]{2,1,0:T(8,128)}, f32[...) custom-call(f32[4,256,256]{2,1,0:T(8,128)} %bitcast.3, ...), custom_call_target="tpu_custom_call" | custom-call | tf_op jit(solution)/shard_map/pallas_call | solution.py:625
  69.3 11.9 %shard_map.38 = f32[1,2,4,256,256]{4,3,2,1,0:T(8,128)} custom-call(f32[4,256,256]{2,1,0:T(8,128)} %bitcast.4, f32[2,256,256]{2,1,0:T(8,128)} %get-tuple-element.13.refs_1_, f32[2,256,256]{2,1,0:T(8,128)} %get-tuple-element.14.refs_2_, f32[4,256,256]{2,1,0:T(8,128)} %bitcast.6, f32[1,256,256]{2,1,0:T(8,128)} %get-tuple-element.15.refs_4_, ...), custom_call_target="tpu_custom_call" | custom-call | tf_op jit(solution)/shard_map/pallas_call | solution.py:648

commit v4 on v3

--- a/solution.py
+++ b/solution.py
@@ -30,13 +30,21 @@
 def pair_table(fine, coarse):
     rows = lax.broadcasted_iota(jnp.int32, (fine, coarse), 0) // 2
     columns = lax.broadcasted_iota(jnp.int32, (fine, coarse), 1)
-    return (rows == columns).astype(F32)
+    return (rows == columns).astype(F32).astype(jnp.bfloat16)
+
+
+def table_dot(value, table):
+    out = None
+    for _ in range(3):
+        part = value.astype(jnp.bfloat16)
+        value = value - part.astype(F32)
+        term = jnp.dot(part, table, preferred_element_type=F32)
+        out = term if out is None else out + term
+    return out
 
 
 def pooled(total, pair, scratch):
-    scratch[...] = jnp.dot(
-        total, pair, precision=lax.Precision.HIGHEST, preferred_element_type=F32
-    )
+    scratch[...] = table_dot(total, pair)
     return scratch[pl.ds(0, 128, stride=2), :] + scratch[pl.ds(1, 128, stride=2), :]
 
 
@@ -57,7 +65,7 @@
             below, here = here, above
 
 
-N_SEND = 256
+N_SEND = 320
 
 
 def chain_kernel(
@@ -66,7 +74,7 @@
     fine_s, fine_r, fine_p, half, own, buf, rate_c, seed, state_a, state_b,
     edge_out, edge_in, found, layer, start, mid, end_state, near_c, warm,
     load_sem, send_sem, slot_sem, fine_sem, seed_sem, rate_sem, edge_sem, state_sem, halo_sem,
-    restart_sem, near_sem, halo_piece,
+    restart_sem, near_sem, rate_half_sem,
 ):
     y, x, c, z = (lax.axis_index(name) for name in AXES)
     chip = y * 4 + x
@@ -122,15 +130,22 @@
     load_s.start()
     load_r.start()
     barrier = pltpu.get_barrier_semaphore()
-    peers = [step(d) for step in (first, second) for d in (1, -1, 2)]
+    plane = [(dy, dx) for dy in range(4) for dx in range(4) if dy or dx]
+    peers = [(turned(y + dy), turned(x + dx), c, z) for dy, dx in plane]
     peers += [(y, x, c, turned(z + d)) for d in (1, 2, 3)]
     peers += [(y, x, 1 - c, turned(z + d)) for d in (0, 1, 2, 3)]
     for device in peers:
         pl.semaphore_signal(barrier, inc=1, device_id=device, device_id_type=MESH)
 
-    @pl.when(jnp.logical_not(is_last))
-    def _():
-        pl.semaphore_signal(barrier, inc=1, device_id=(3, 3, 1, z), device_id_type=MESH)
+    def greet(step):
+        to = (3, 3, 1, turned(z + step))
+        pl.semaphore_signal(barrier, inc=1, device_id=to, device_id_type=MESH)
+
+    pl.when(jnp.logical_not(is_last))(lambda: greet(0))
+    pl.when(z > 0)(lambda: greet(-1))
+    pl.when(z < 3)(lambda: greet(1))
+    inner_z = (z > 0) & (z < 3)
+    more = jnp.where(is_last, jnp.where(inner_z, 95, 63), 0)
 
     pair = pair_table(256, 128)
 
@@ -145,7 +160,7 @@
     pl.when(is_last)(lambda: restrict(fine_p, 2, 0.125))
     load_s.wait()
     restrict(fine_s, 0, 0.0625)
-    pl.semaphore_wait(barrier, jnp.where(is_last, len(peers) + 31, len(peers)))
+    pl.semaphore_wait(barrier, len(peers) + more)
 
     layers = pl.ds(2 * z, 2)
     rows = pl.ds(16 * c, 48)
@@ -182,32 +197,90 @@
             z > 0,
         )
 
+    def along_z(pieces, sems, index):
+        for (src, dst), n, step, cond in zip(pieces, (0, 1), (1, -1), (z < 3, z > 0)):
+            send(src, dst, sems.at[index, n], (y, x, c, turned(z + step)), cond)
+
     def other_halos():
-        for f in range(2):
-            for n, step, cond in ((0, 1, z < 3), (1, -1, z > 0)):
+        src = own.at[0, :, pl.ds(16, 128), :]
+        along_z([(src, near_c.at[0, pl.ds(4 * n, 2)]) for n in range(2)], near_sem, 0)
+        fine_halo(source, source_lo, source_hi, 1, 2)
+
+    rate_rows = pl.ds(128 * c, 128)
+    rate_views = [view.at[:, rate_rows, :] for view in (rate_lo, rate_hi)]
+    rate_c_views = [near_c.at[1, pl.ds(4 * n + c, 1)] for n in range(2)]
+    rate_others = [view.at[:, pl.ds(128 * (1 - c), 128), :] for view in (rate_lo, rate_hi)]
+    rate_c_others = [near_c.at[1, pl.ds(4 * n + 1 - c, 1)] for n in range(2)]
+
+    def rate_fine():
+        srcs = [rate.at[pl.ds(3 * (1 - n), 1), rate_rows, :] for n in range(2)]
+        along_z(zip(srcs, rate_views), rate_half_sem, 0)
+
+    def rate_coarse():
+        src = own.at[1, pl.ds(c, 1), pl.ds(16, 128), :]
+        along_z([(src, view) for view in rate_c_views], near_sem, 1)
+
+    def rate_across():
+        for views, sems, index in ((rate_c_views, near_sem, 1), (rate_views, rate_half_sem, 0)):
+            for n, cond in ((0, z > 0), (1, z < 3)):
+                arrived(views[n], sems.at[index, n], cond)
+                send(views[n], views[n], rate_half_sem.at[1 + index, n], partner, cond)
+
+    fine_halo(prev, prev_lo, prev_hi, 2, 0)
+
+    def fine_own():
+        for n in range(30, -1, -1):
+            send(
+                fine_p.at[:, pl.ds(8 * n, 8), :], restart.at[pl.ds(2, 4), n // 2, n % 2],
+                fine_sem.at[0, n], (n // 8, n // 2 % 4, n % 2, z), is_last,
+            )
+
+        @pl.when(is_last)
+        def _():
+            local = pltpu.make_async_copy(
+                fine_p.at[:, pl.ds(248, 8), :], restart.at[pl.ds(2, 4), 15, 1], load_sem.at[0]
+            )
+            local.start()
+            local.wait()
+
+    def fine_beside():
+        for n in range(31, -1, -1):
+            for low, to, step, index, cond in (
+                (2, 0, 1, 1, is_last & (z < 3)),
+                (0, 6, -1, 2, is_last & (z > 0)),
+            ):
                 send(
-                    own.at[f, :, pl.ds(16, 128), :], near_c.at[f, pl.ds(4 * n, 2)],
-                    near_sem.at[f, n], (y, x, c, turned(z + step)), cond,
+                    fine_p.at[pl.ds(low, 2), pl.ds(8 * n, 8), :],
+                    restart.at[pl.ds(to, 2), n // 2, n % 2], fine_sem.at[index, n],
+                    (n // 8, n // 2 % 4, n % 2, turned(z + step)), cond,
                 )
-        fine_halo(source, source_lo, source_hi, 1, 2)
-        fine_halo(rate, rate_lo, rate_hi, 1, 4)
-
-    fine_halo(prev, prev_lo, prev_hi, 2, 0)
-
-    for n in range(31):
-        send(
-            fine_p.at[:, pl.ds(8 * n, 8), :], restart.at[pl.ds(2, 4), n // 2, n % 2],
-            fine_sem.at[n], (n // 8, n // 2 % 4, n % 2, z), is_last,
-        )
-
-    @pl.when(is_last)
-    def _():
-        local = pltpu.make_async_copy(
-            fine_p.at[:, pl.ds(248, 8), :], restart.at[pl.ds(2, 4), 15, 1], load_sem.at[0]
-        )
-        local.start()
-        local.wait()
-
+
+    fine_parts = (
+        (0, 2, 4, jnp.logical_not(is_last), None), (1, 0, 2, z > 0, z > 0), (2, 6, 2, z < 3, z < 3)
+    )
+
+    def fine_direct(index):
+        _, low, count, ready_cond, cond = fine_parts[index]
+        view = restart.at[pl.ds(low, count), chip, c]
+        arrived(view, fine_sem.at[index, mine], ready_cond)
+        for dy, dx in plane:
+            to = (turned(y + dy), turned(x + dx), c, z)
+            send(view, view, fine_sem.at[index, mine], to, cond)
+
+    def fine_across():
+        for index, low, count, _, cond in fine_parts:
+            for dy, dx in plane:
+                other = turned(y + dy) * 4 + turned(x + dx)
+                view = restart.at[pl.ds(low, count), other, c]
+                arrived(view, fine_sem.at[index, other * 2 + c], cond)
+            view = restart.at[pl.ds(low, count), :, c]
+            send(view, view, restart_sem.at[index], partner, cond)
+
+    def fine_ready():
+        for index, low, count, _, cond in fine_parts:
+            arrived(restart.at[pl.ds(low, count), :, 1 - c], restart_sem.at[index], cond)
+
+    fine_own()
     load_r.wait()
     restrict(fine_r, 1, 0.0625)
     for d in (1, 3, 2):
@@ -235,9 +308,9 @@
     def chunk(da, db):
         return buf.at[slot(da, db)], slot_sem.at[slot(da, db)]
 
-    def across_chip(da, db):
+    def across_chip(da, db, cond=None):
         view = buf.at[slot(da, db), :, pl.ds(16 * (1 - c), 48), :]
-        send(view, view, slot_sem.at[slot(da, db)], partner)
+        send(view, view, slot_sem.at[slot(da, db)], partner, cond)
 
     def onward(da, db):
         full, sem = chunk(da, db)
@@ -251,28 +324,6 @@
         view = buf.at[slot(da, db), pl.ds(4 * h, 4)]
         send(view, view, sem, device)
 
-    def fine(da, db):
-        here = slot(da, db)
-        return restart.at[pl.ds(2, 4), here // 2, c], fine_sem.at[here]
-
-    def fine_onward(da, db):
-        full, sem = fine(da, db)
-        for step in (1, -1):
-            send(full, full, sem, second(step))
-
-    def fine_relay(da, db, device, h):
-        full, sem = fine(da, db)
-        arrived(full, sem)
-        view = restart.at[pl.ds(2 + 2 * h, 2), slot(da, db) // 2, c]
-        send(view, view, sem, device)
-
-    def fine_own():
-        full, sem = fine(0, 0)
-        arrived(full, sem, jnp.logical_not(is_last))
-        for step in (1, -1):
-            send(full, full, sem, first(step))
-        fine_onward(0, 0)
-
     def near(relay, onward):
         relay(-1, 0, first(1), 0)
         onward(-1, 0)
@@ -282,37 +333,36 @@
     def ring(relay, a):
         for step, h in ((-1, 0), (1, 1)):
             relay(a, step, second(-step), h)
-            if relay is not fine_relay:
-                across_chip(a, step)
+            across_chip(a, step)
 
     full, sem = chunk(0, 0)
     arrived(full.at[pl.ds(0, 6)], sem)
     for step in (1, -1):
         send(full, full, sem, first(step))
     onward(0, 0)
-    fine_own()
     near(relay, onward)
     spread_seed()
     other_halos()
     ring(relay, 0)
-    near(fine_relay, fine_onward)
     arrived(*chunk(2, 0))
     onward(2, 0)
     ring(relay, -1)
     ring(relay, 1)
-    ring(fine_relay, 0)
-    arrived(*fine(2, 0))
-    fine_onward(2, 0)
     arrived(*chunk(0, 2))
     across_chip(0, 2)
     ring(relay, 2)
-    for a in (-1, 1, 2):
-        arrived(*chunk(a, 2))
-        across_chip(a, 2)
-    for a in range(4):
+    fine_beside()
+
+    def ready(block):
+        for a in (-1, 1, 2):
+            here = slot(a, 2)
+            cond = here // 8 == block
+            arrived(*chunk(a, 2), cond)
+            across_chip(a, 2, cond)
         for b in range(4):
-            other = (a * 4 + b) * 2 + 1 - c
+            other = (block * 4 + b) * 2 + 1 - c
             arrived(buf.at[other, :, rows, :], slot_sem.at[other])
+
     arrived(rate_c.at[pl.ds(0, 6)], rate_sem)
     arrived(seed.at[pl.ds(0, 7)], seed_sem.at[1])
 
@@ -355,20 +405,12 @@
             send(edge_out.at[e], edge_in.at[e, 0], edge_sem.at[e, 0], up, active)
             send(edge_out.at[e], edge_in.at[e, 1], edge_sem.at[e, 1], down, active)
             if block == 1:
-                for a in (-1, 1, 2):
-                    ring(fine_relay, a)
-                for a in (0, -1, 1, 2):
-                    arrived(*fine(a, 2))
-                view = restart.at[pl.ds(2, 4), :, c]
-                send(view, view, restart_sem.at[0], partner)
-            for piece in ((0,), (1, 2), (3,))[e]:
-                for low, to, step, index in ((2, 6, -1, 1), (4, 0, 1, 2)):
-                    some = pl.ds(4 * piece, 4)
-                    send(
-                        restart.at[pl.ds(low, 2), some, c], restart.at[pl.ds(to, 2), some, c],
-                        halo_piece.at[index - 1, piece], (y, x, c, turned(z + step)),
-                        (z > 0) if step < 0 else (z < 3),
-                    )
+                rate_fine()
+                fine_direct(0)
+            if block == 2:
+                rate_coarse()
+                fine_direct(1)
+                fine_direct(2)
             arrived(edge_in.at[e, 0], edge_sem.at[e, 0], active)
             arrived(edge_in.at[e, 1], edge_sem.at[e, 1], active)
 
@@ -377,6 +419,7 @@
                 state_a[pl.ds(1, 8), pl.ds(40, 16), :] = edge_in[e, 1]
 
             pl.when(active)(spill)
+        ready(block)
         count = jnp.where(y > block, 8, jnp.where(active, 2 * x + 1, 0))
         run(block, 0, jnp.minimum(count, 4), range(6))
         run(block, 4, jnp.maximum(count - 4, 0), range(1, 5))
@@ -395,6 +438,7 @@
                     found.at[core, pl.ds(low, count)], start.at[pl.ds(3 + low, count), here, :],
                     state_sem, (y, x, core, to), cond if d else cond & (c != core),
                 )
+    rate_across()
     zero = jnp.zeros((3, 144, 128), F32)
     start[pl.ds(0, 3)] = zero
     start[pl.ds(11, 3)] = zero
@@ -416,8 +460,10 @@
         warm[3 * n] = 0.125 * pooled(fine_r[2 * n] + fine_r[2 * n + 1], pair, half)
     for f in range(2):
         near_c[f, pl.ds(2, 2)] = own[f, :, pl.ds(16, 128), :]
-        for n, cond in ((0, z > 0), (1, z < 3)):
-            arrived(near_c.at[f, pl.ds(4 * n, 2)], near_sem.at[f, n], cond)
+    for n, cond in ((0, z > 0), (1, z < 3)):
+        arrived(near_c.at[0, pl.ds(4 * n, 2)], near_sem.at[0, n], cond)
+        arrived(rate_c_others[n], rate_half_sem.at[2, n], cond)
+    fine_across()
     for count, cond in ((5, (z == 0) | (z == 3)), (7, (z == 1) | (z == 2))):
         arrived(start.at[pl.ds(0, count), pl.ds(0, 112), :], state_sem, cond)
 
@@ -466,25 +512,20 @@
     states[1] = mid[pl.ds(1, 4), pl.ds(8, 128), :] - warm[...]
     states[2] = end_state[:, pl.ds(8, 128), :] - warm[...]
 
-    for low, index, cond in ((6, 1, z < 3), (0, 2, z > 0)):
-        for piece in range(4):
-            view = restart.at[pl.ds(low, 2), pl.ds(4 * piece, 4), c]
-            arrived(view, halo_piece.at[index - 1, piece], cond)
-        view = restart.at[pl.ds(low, 2), :, c]
-        send(view, view, restart_sem.at[index + 2], partner, cond)
-    for low, index, cond in ((6, 3, z < 3), (0, 4, z > 0)):
-        arrived(restart.at[pl.ds(low, 2), :, 1 - c], restart_sem.at[index], cond)
-    arrived(restart.at[pl.ds(2, 4), :, 1 - c], restart_sem.at[0])
-    for index, view in enumerate((source_lo, source_hi, rate_lo, rate_hi)):
-        arrived(view, halo_sem.at[index + 2], (z > 0) if index % 2 == 0 else (z < 3))
+    fine_ready()
+    for n, cond in ((0, z > 0), (1, z < 3)):
+        arrived((source_lo, source_hi)[n], halo_sem.at[2 + n], cond)
+        arrived(rate_others[n], rate_half_sem.at[1, n], cond)
+    assert len(waits) <= N_SEND
     for cond, wait in waits:
         guarded(cond, wait)
 
 
 def fine_kernel(*refs):
-    inputs, out = refs[:11], refs[11]
+    inputs, result = refs[:11], refs[11]
     half, lifted, mixed, base, extra, last, later = refs[12:19]
     held, load_sem = refs[19:30], refs[30]
+    out, store_sem = refs[31], refs[32]
     loads = [
         pltpu.make_async_copy(a, b, load_sem.at[n]) for n, (a, b) in enumerate(zip(inputs, held))
     ]
@@ -497,7 +538,7 @@
     spread = (
         lax.broadcasted_iota(jnp.int32, (128, 256), 0)
         == lax.broadcasted_iota(jnp.int32, (128, 256), 1) // 2
-    ).astype(F32)
+    ).astype(F32).astype(jnp.bfloat16)
 
     def prev_layer(k):
         return prev_lo.at[k] if k < 2 else prev_hi.at[k - 6] if k > 5 else prev.at[k - 2]
@@ -513,18 +554,22 @@
         return value if cond is None else jnp.where(cond, value, 0.0)
 
     loads[10].wait()
+
+    def lift(n, change):
+        wide = table_dot(change.reshape(512, 128), spread)
+        for k in range(4):
+            for h in range(2):
+                column = wide[128 * k : 128 * k + 128, 128 * h : 128 * h + 128]
+                lifted[n, k, h, pl.ds(0, 128, stride=2), :] = column
+                lifted[n, k, h, pl.ds(1, 128, stride=2), :] = column
+
+    lift(1, states[1])
+    lift(2, states[2])
     loads[9].wait()
     for k in range(4):
         seed_c = 0.125 * pooled(restart[2 * k] + restart[2 * k + 1], pair, half)
-        for n in range(3):
-            change = states[n, k] if n else states[n, k] - seed_c
-            wide = jnp.dot(
-                change, spread, precision=lax.Precision.HIGHEST, preferred_element_type=F32
-            )
-            for h in range(2):
-                column = wide[:, 128 * h : 128 * h + 128]
-                lifted[n, k, h, pl.ds(0, 128, stride=2), :] = column
-                lifted[n, k, h, pl.ds(1, 128, stride=2), :] = column
+        states[0, k] = states[0, k] - seed_c
+    lift(0, states[0])
 
     def share(v):
         return v * pl.reciprocal(1.0 + v * v)
@@ -596,6 +641,10 @@
 
     lax.fori_loop(0, 32, node_one, 0, unroll=4)
     wrap(later, 6)
+    stores = [
+        pltpu.make_async_copy(out.at[0, n], result.at[0, n], store_sem.at[n]) for n in range(2)
+    ]
+    stores[0].start()
 
     def node_two(i, carry):
         r = pl.ds(8 * i, 8)
@@ -607,6 +656,9 @@
         return carry
 
     lax.fori_loop(0, 32, node_two, 0, unroll=4)
+    stores[1].start()
+    for copy in stores:
+        copy.wait()
 
 
 def shards(previous_end, source, rate):
@@ -636,8 +688,8 @@
             scratch(3, 8, 16, 128), scratch(3, 2, 8, 16, 128), scratch(2, 8, 16, 128),
             scratch(160, 128), scratch(14, 144, 128), scratch(6, 144, 128), scratch(4, 144, 128),
             scratch(2, 6, 128, 128), scratch(4, 128, 128),
-            dma((3,)), dma((N_SEND,)), dma((32,)), dma((32,)), dma((2,)), dma, dma((3, 2)), dma,
-            dma((6,)), dma((5,)), dma((2, 2)), dma((2, 4)),
+            dma((3,)), dma((N_SEND,)), dma((32,)), dma((3, 32)), dma((2,)), dma, dma((3, 2)), dma,
+            dma((4,)), dma((3,)), dma((2, 2)), dma((3, 2)),
         ],
         compiler_params=pltpu.CompilerParams(
             collective_id=0, has_side_effects=True, vmem_limit_bytes=63 * 1024 * 1024
@@ -649,7 +701,7 @@
         fine_kernel,
         out_shape=shape(1, 2, 4, 256, 256),
         in_specs=[any_space] * 11,
-        out_specs=vmem,
+        out_specs=any_space,
         scratch_shapes=[
             scratch(256, 128), scratch(3, 4, 2, 256, 128), scratch(8, 2, 272, 128),
             scratch(6, 256, 256), scratch(6, 256, 256), scratch(4, 256, 256),
@@ -658,6 +710,7 @@
             scratch(4, 256, 256), scratch(1, 256, 256), scratch(1, 256, 256),
             scratch(4, 256, 256), scratch(1, 256, 256), scratch(1, 256, 256),
             scratch(8, 256, 256), scratch(3, 4, 128, 128), dma((11,)),
+            scratch(1, 2, 4, 256, 256), dma((2,)),
         ],
         compiler_params=pltpu.CompilerParams(vmem_limit_bytes=63 * 1024 * 1024),
     )(prev, prev_lo, prev_hi, own, source_lo, source_hi, rate, rate_lo, rate_hi, restart, states)

time: 81.8 us -> 78.5 us (0.960)
  Pallas kernels: 81.2 us -> 78.4 us
    pallas_call x1, Pallas kernels: 11.9 us -> 9.43 us  [shards(): pl.pallas_call(fine_kernel, out_shape=shape(1, 2, 4, 256, 256), in_specs=...]
where the time goes in v4:
time: 78.5 us; the launch traced here: 78.4 us
  Pallas kernels  78.4 us (100%)
    pallas_call x1, Pallas kernels, shards(): pl.pallas_call(chain_kernel, out_shape=[shape(3, 4, 128, 128), shape(8, 1...  68.9 us
    pallas_call x1, Pallas kernels, shards(): pl.pallas_call(fine_kernel, out_shape=shape(1, 2, 4, 256, 256), in_specs=...  9.43 us

profile of v4, /device:TPU:29, one launch (start us, length us, event | category | flops | bytes accessed | tf_op | source)
XLA Modules:
  0.0 78.4 jit_solution(3259909045175303086)
XLA Ops:
  0.0 68.9 %shard_map.37 = (f32[3,4,128,128]{3,2,1,0:T(8,128)}, f32[8,16,2,8,256]{4,3,2,1,0:T(8,128)}, f32[2,256,256]{2,1,0:T(8,128)}, f32[2,256,256]{2,1,0:T(8,128)}, f32[...) custom-call(f32[4,256,256]{2,1,0:T(8,128)} %bitcast.3, ...), custom_call_target="tpu_custom_call" | custom-call | tf_op jit(solution)/shard_map/pallas_call | solution.py:677
  68.9 9.4 %shard_map.38 = f32[1,2,4,256,256]{4,3,2,1,0:T(8,128)} custom-call(f32[4,256,256]{2,1,0:T(8,128)} %bitcast.4, f32[2,256,256]{2,1,0:T(8,128)} %get-tuple-element.13.refs_1_, f32[2,256,256]{2,1,0:T(8,128)} %get-tuple-element.14.refs_2_, f32[4,256,256]{2,1,0:T(8,128)} %bitcast.6, f32[1,256,256]{2,1,0:T(8,128)} %get-tuple-element.15.refs_4_, ...), custom_call_target="tpu_custom_call" | custom-call | tf_op jit(solution)/shard_map/pallas_call | solution.py:700

commit v5 on v4

--- a/solution.py
+++ b/solution.py
@@ -351,7 +351,6 @@
     arrived(*chunk(0, 2))
     across_chip(0, 2)
     ring(relay, 2)
-    fine_beside()
 
     def ready(block):
         for a in (-1, 1, 2):
@@ -406,10 +405,12 @@
             send(edge_out.at[e], edge_in.at[e, 1], edge_sem.at[e, 1], down, active)
             if block == 1:
                 rate_fine()
+                fine_beside()
                 fine_direct(0)
             if block == 2:
                 rate_coarse()
                 fine_direct(1)
+            if block == 3:
                 fine_direct(2)
             arrived(edge_in.at[e, 0], edge_sem.at[e, 0], active)
             arrived(edge_in.at[e, 1], edge_sem.at[e, 1], active)

time: 78.5 us -> 78 us (level)
  no operation moved by 1% of the time
where the time goes in v5:
time: 78 us; the launch traced here: 77.9 us
  Pallas kernels  77.8 us (100%)
    pallas_call x1, Pallas kernels, shards(): pl.pallas_call(chain_kernel, out_shape=[shape(3, 4, 128, 128), shape(8, 1...  68.4 us
    pallas_call x1, Pallas kernels, shards(): pl.pallas_call(fine_kernel, out_shape=shape(1, 2, 4, 256, 256), in_specs=...  9.43 us

profile of v5, /device:TPU:29, one launch (start us, length us, event | category | flops | bytes accessed | tf_op | source)
XLA Modules:
  0.0 77.9 jit_solution(5462559782308536320)
XLA Ops:
  0.0 68.4 %shard_map.37 = (f32[3,4,128,128]{3,2,1,0:T(8,128)}, f32[8,16,2,8,256]{4,3,2,1,0:T(8,128)}, f32[2,256,256]{2,1,0:T(8,128)}, f32[2,256,256]{2,1,0:T(8,128)}, f32[...) custom-call(f32[4,256,256]{2,1,0:T(8,128)} %bitcast.3, ...), custom_call_target="tpu_custom_call" | custom-call | tf_op jit(solution)/shard_map/pallas_call | solution.py:678
  68.4 9.4 %shard_map.38 = f32[1,2,4,256,256]{4,3,2,1,0:T(8,128)} custom-call(f32[4,256,256]{2,1,0:T(8,128)} %bitcast.4, f32[2,256,256]{2,1,0:T(8,128)} %get-tuple-element.13.refs_1_, f32[2,256,256]{2,1,0:T(8,128)} %get-tuple-element.14.refs_2_, f32[4,256,256]{2,1,0:T(8,128)} %bitcast.6, f32[1,256,256]{2,1,0:T(8,128)} %get-tuple-element.15.refs_4_, ...), custom_call_target="tpu_custom_call" | custom-call | tf_op jit(solution)/shard_map/pallas_call | solution.py:701

commit v6 on v5

--- a/solution.py
+++ b/solution.py
@@ -640,7 +640,7 @@
             put(later, k, i, 0.5 * value + extra[k, r, :])
         return carry
 
-    lax.fori_loop(0, 32, node_one, 0, unroll=4)
+    lax.fori_loop(0, 32, node_one, 0, unroll=8)
     wrap(later, 6)
     stores = [
         pltpu.make_async_copy(out.at[0, n], result.at[0, n], store_sem.at[n]) for n in range(2)
@@ -656,7 +656,7 @@
             out[0, 1, k, r, :] = value + linear(later, k + 1, i, *planes[k : k + 3])
         return carry
 
-    lax.fori_loop(0, 32, node_two, 0, unroll=4)
+    lax.fori_loop(0, 32, node_two, 0, unroll=8)
     stores[1].start()
     for copy in stores:
         copy.wait()

time: 78 us -> 77.5 us (level)
  no operation moved by 1% of the time
where the time goes in v6:
time: 77.5 us; the launch traced here: 77.4 us
  Pallas kernels  77.3 us (100%)
    pallas_call x1, Pallas kernels, shards(): pl.pallas_call(chain_kernel, out_shape=[shape(3, 4, 128, 128), shape(8, 1...  68.4 us
    pallas_call x1, Pallas kernels, shards(): pl.pallas_call(fine_kernel, out_shape=shape(1, 2, 4, 256, 256), in_specs=...  8.94 us

profile of v6, /device:TPU:29, one launch (start us, length us, event | category | flops | bytes accessed | tf_op | source)
XLA Modules:
  0.0 77.4 jit_solution(17269865688994639239)
XLA Ops:
  0.0 68.4 %shard_map.37 = (f32[3,4,128,128]{3,2,1,0:T(8,128)}, f32[8,16,2,8,256]{4,3,2,1,0:T(8,128)}, f32[2,256,256]{2,1,0:T(8,128)}, f32[2,256,256]{2,1,0:T(8,128)}, f32[...) custom-call(f32[4,256,256]{2,1,0:T(8,128)} %bitcast.3, ...), custom_call_target="tpu_custom_call" | custom-call | tf_op jit(solution)/shard_map/pallas_call | solution.py:678
  68.4 8.9 %shard_map.38 = f32[1,2,4,256,256]{4,3,2,1,0:T(8,128)} custom-call(f32[4,256,256]{2,1,0:T(8,128)} %bitcast.4, f32[2,256,256]{2,1,0:T(8,128)} %get-tuple-element.13.refs_1_, f32[2,256,256]{2,1,0:T(8,128)} %get-tuple-element.14.refs_2_, f32[4,256,256]{2,1,0:T(8,128)} %bitcast.6, f32[1,256,256]{2,1,0:T(8,128)} %get-tuple-element.15.refs_4_, ...), custom_call_target="tpu_custom_call" | custom-call | tf_op jit(solution)/shard_map/pallas_call | solution.py:701
